TPU v7x, 128 devices: a whole 4x4x4 slice. The times are simulated.
128 devices in a mesh: space: 16 (over z_lo, y, core), group: 8 (over z_hi, x).
Axes of the slice: x: 4, y: 4, z: 4 (z_hi: 2, z_lo: 2; z = z_hi * 2 + z_lo), core: 2. Of those that a mesh axis runs over, the one named last changes fastest.
Arguments:
- snapshot_basis: bfloat16 [131072, 2048], P('space', 'group'), may hold values from -40 to 40
- sketch: float32 [3, 512, 256], replicated, may hold values from -0.25 to 0.25
Outputs:
- merged_basis: bfloat16 [131072, 256], P(('space', 'group'))
All inputs are finite; a program needn't handle non-finite values.
Results may differ from a plain program's by a relative error of at most 0.0067.
Values may be sent and summed in bfloat16 or wider, within the bound.
A program may use at most 128 MiB of HBM per device.

v0:
```python
import jax
import jax.numpy as jnp
from jax import lax
from jax.sharding import PartitionSpec as P

STEPS = 5


def from_partner(block, axis, bit):
    count = lax.axis_size(axis)
    route = []
    for low in range(count):
        high = low | 1 << bit
        if high != low and high < count:
            route += [(low, high), (high, low)]
    return lax.ppermute(block, axis, route)


def split_up(value, dim, count):
    before, after = (value.shape[:dim], value.shape[dim + 1 :])
    return jnp.moveaxis(value.reshape(*before, count, -1, *after), dim, 0)


def summed_on_arrival(value, axis, dim):
    pieces = split_up(value, dim, lax.axis_size(axis))
    arrived = lax.all_to_all(pieces, axis, split_axis=0, concat_axis=0, tiled=True)
    return arrived.sum(axis=0)


def padded_to(lines, count):
    spare = -lines.shape[0] % count
    if not spare:
        return lines
    return jnp.concatenate([lines, jnp.zeros((spare, *lines.shape[1:]), lines.dtype)])


def in_order(pieces, dim):
    pieces = jnp.moveaxis(pieces, 0, dim)
    lengths = pieces.shape
    return pieces.reshape(*lengths[:dim], lengths[dim] * lengths[dim + 1], *lengths[dim + 2 :])


def sent_to_all(value, axis):
    copies = jnp.broadcast_to(value, (lax.axis_size(axis), *value.shape))
    return lax.all_to_all(copies, axis, split_axis=0, concat_axis=0, tiled=True)


def gather_directly(value, axis, dim):
    return in_order(sent_to_all(value, axis), dim)


def nested_sum(value, axes):
    lines = value.reshape(-1)
    own = summed_on_arrival(padded_to(lines, lax.axis_size(axes)), axes, 0)
    whole = gather_directly(own, axes, 0)
    return whole[: len(lines)].reshape(value.shape)


def filter_mix(gram, sketch_level):
    width = gram.shape[0]
    eye = jnp.eye(width, dtype=jnp.float32)
    scaled = gram / (jnp.trace(gram) / width)
    shifted = scaled - eye
    iterate = shifted / (1.0 + jnp.sqrt(jnp.sum(shifted * shifted)))
    for step in range(STEPS):
        square = jnp.dot(iterate, iterate, precision=lax.Precision.HIGHEST)
        cube = jnp.dot(square, iterate, precision=lax.Precision.HIGHEST)
        iterate = 1.5 * iterate - 0.5 * cube
    applied = jnp.dot(iterate, sketch_level, precision=lax.Precision.HIGHEST)
    return (0.5 * (sketch_level + applied)).astype(jnp.bfloat16)


def local_gram(stacked):
    return lax.dot_general(
        stacked, stacked, (((0,), (0,)), ((), ())), preferred_element_type=jnp.float32
    )


def body(snapshot_basis, sketch):
    width = snapshot_basis.shape[1]
    rows = snapshot_basis.shape[0]
    groups = lax.axis_size("group")
    levels = groups.bit_length() - 1
    member = lax.axis_index("group")
    block_rows = rows // groups
    own_panel = snapshot_basis
    for level in range(levels):
        other = from_partner(own_panel, "group", level)
        upper = member >> level & 1 == 1
        lower_part = jnp.where(upper, other, own_panel)
        upper_part = jnp.where(upper, own_panel, other)
        stacked = jnp.concatenate([lower_part, upper_part], axis=1)
        gram = nested_sum(local_gram(stacked), "space")
        mix = filter_mix(gram, sketch[level])
        own_panel = jnp.dot(stacked, mix, preferred_element_type=jnp.float32).astype(jnp.bfloat16)
    blocks = own_panel.reshape(groups, block_rows, width)
    return lax.dynamic_index_in_dim(blocks, member, 0, keepdims=False)


def solution(mesh):
    in_specs = (P("space", "group"), P())
    out_specs = P(("space", "group"), None)
    return jax.shard_map(body, mesh=mesh, in_specs=in_specs, out_specs=out_specs, check_vma=False)
```

profile of v0, /device:TPU:1, one launch (start us, length us, event | category | flops | bytes accessed | tf_op | source)
XLA Modules:
  0.0 573.9 jit_solution(13401689399837880580)
XLA Ops:
  0.0 2.0 collective-permute-start
  2.0 90.2 %collective-permute-done = bf16[8192,256]{1,0:T(8,128)(2,1)} collective-permute-done((bf16[8192,256]{1,0:T(8,128)(2,1)}, bf16[8192,256]{1,0:T(8,128)(2,1)}, u32[]{:S(2)}, u32[]{:S(2)}) %collective-permute-start) | collective-permute-done | bytes 4194336 | tf_op jit(solution)/shard_map/ppermute | solution.py:16
  92.2 3.8 broadcast_select_fusion.1
  96.0 1.9 copy-done.2
  99.2 4.5 fusion.2
  105.0 22.7 %all_to_all.57 = f32[16,1,16384]{2,1,0:T(1,128)S(1)} all-to-all(f32[16,1,16384]{2,1,0:T(1,128)S(1)} %all_to_all.48), channel_id=1, replica_groups=mesh['space'=16,'group'=8] {'space'}, dimensions={0} | all-to-all | bytes 2097152 | tf_op jit(solution)/shard_map/all_to_all | solution.py:26
  128.3 1.9 broadcast_in_dim.15
  130.2 5.2 all-to-all-start.1
  136.8 1.6 copy.9
  138.4 12.8 %all-to-all-done.1 = f32[16,1,16384]{2,1,0:T(1,128)S(1)} async-done(((f32[16,1,16384]{2,1,0:T(1,128)}), f32[16,1,16384]{2,1,0:T(1,128)S(1)}, u32[]{:S(2)}, u32[]{:S(2)}) %all-to-all-start.1) | async-done | bytes 1048608 | tf_op jit(solution)/shard_map/all_to_all | solution.py:45
  151.2 2.5 fusion.35
  156.2 7.0 %fusion.56 = (f32[16,16384]{1,0:T(8,128)S(1)}, f32[16,16384]{1,0:T(8,128)}) fusion(f32[]{:T(128)S(6)} %add.34, s32[16,1,16384]{2,1,0:T(1,128)S(1)} %iota.278, s32[16384]{0:T(1024)S(1)} %bitcast.104, f32[16,1,16384]{2,1,0:T(1,128)S(1)} %all-to-all-done.1, f32[]{:T(128)S(6)} %div.117), kind=kLoop, calls=%fused_computation.107 | loop fusion | flops 1310720 | bytes 4259848 | tf_op jit(solution)/shard_map/div | solution.py:62
  164.6 2.9 fusion.57
  167.7 3.2 fusion.17
  170.9 1.8 fusion.58
  172.8 1.9 fusion.16
  174.6 1.8 fusion.59
  176.5 1.9 fusion.15
  178.3 1.8 fusion.60
  180.2 2.3 fusion.14
  182.6 1.8 fusion.61
  184.4 1.9 fusion.13
  186.3 2.0 fusion.23
  188.3 4.0 convolution_convert_fusion.2
  192.3 2.7 collective-permute-start.1
  195.1 90.5 %collective-permute-done.1 = bf16[8192,256]{0,1:T(8,128)(2,1)} collective-permute-done((bf16[8192,256]{0,1:T(8,128)(2,1)}, bf16[8192,256]{0,1:T(8,128)(2,1)}, u32[]{:S(2)}, u32[]{:S(2)}) %collective-permute-start.1) | collective-permute-done | bytes 4194336 | tf_op jit(solution)/shard_map/ppermute | solution.py:16
  285.5 5.9 %broadcast_select_fusion.3 = (bf16[8192,256]{0,1:T(8,128)(2,1)}, bf16[8192,256]{0,1:T(8,128)(2,1)}) fusion(bf16[8192,256]{0,1:T(8,128)(2,1)} %collective-permute-done.1, bf16[8192,256]{0,1:T(8,128)(2,1)} %convolution_convert_fusion.2, pred[]{:T(512)S(6)} %eq.66), kind=kLoop, calls=%fused_computation.13 | loop fusion | flops 4194304 | bytes 16777216 | tf_op jit(solution)/shard_map/jit(_where)/select_n | solution.py:90
  291.5 10.4 %fusion.1 = f32[512,512]{1,0:T(8,128)S(1)} fusion(bf16[8192,256]{0,1:T(8,128)(2,1)} %get-tuple-element.16, bf16[8192,256]{0,1:T(8,128)(2,1)} %get-tuple-element.15), kind=kOutput, calls=%fused_computation.7 | convolution fusion | flops 4311744512 | bytes 9437184 | tf_op jit(solution)/shard_map/dot_general | solution.py:74
  303.1 19.3 %all_to_all.58 = f32[16,1,16384]{2,1,0:T(1,128)S(1)} all-to-all(f32[16,1,16384]{2,1,0:T(1,128)S(1)} %all_to_all.49), channel_id=1, replica_groups=mesh['space'=16,'group'=8] {'space'}, dimensions={0} | all-to-all | bytes 2097152 | tf_op jit(solution)/shard_map/all_to_all | solution.py:26
  323.9 19.1 %all_to_all.59 = f32[16,1,16384]{2,1,0:T(1,128)S(1)} all-to-all(f32[16,1,16384]{2,1,0:T(1,128)S(1)} %broadcast_in_dim.17), channel_id=1, replica_groups=mesh['space'=16,'group'=8] {'space'}, dimensions={0} | all-to-all | bytes 2097152 | tf_op jit(solution)/shard_map/all_to_all | solution.py:45
  346.7 6.9 %fusion.55 = (f32[16,16384]{1,0:T(8,128)S(1)}, f32[16,16384]{1,0:T(8,128)}) fusion(f32[]{:T(128)S(6)} %add.36, s32[16,1,16384]{2,1,0:T(1,128)S(1)} %iota.278, s32[16384]{0:T(1024)S(1)} %bitcast.105, f32[16,1,16384]{2,1,0:T(1,128)S(1)} %all_to_all.59, f32[]{:T(128)S(6)} %div.128), kind=kLoop, calls=%fused_computation.106 | loop fusion | flops 1310720 | bytes 4259848 | tf_op jit(solution)/shard_map/div | solution.py:62
  355.0 2.8 fusion.62
  358.0 3.2 fusion.12
  361.2 1.8 fusion.63
  363.1 1.9 fusion.11
  364.9 1.8 fusion.64
  366.8 1.9 fusion.10
  368.6 1.8 fusion.65
  370.5 2.3 fusion.9
  372.8 1.8 fusion.66
  374.7 1.9 fusion.8
  376.5 2.0 fusion.22
  378.6 4.1 convolution_convert_fusion.1
  382.7 3.3 collective-permute-start.2
  386.0 89.8 %collective-permute-done.2 = bf16[8192,256]{0,1:T(8,128)(2,1)} collective-permute-done((bf16[8192,256]{0,1:T(8,128)(2,1)}, bf16[8192,256]{0,1:T(8,128)(2,1)}, u32[]{:S(2)}, u32[]{:S(2)}) %collective-permute-start.2) | collective-permute-done | bytes 4194336 | tf_op jit(solution)/shard_map/ppermute | solution.py:16
  475.8 5.9 %broadcast_select_fusion.5 = (bf16[8192,256]{0,1:T(8,128)(2,1)}, bf16[8192,256]{0,1:T(8,128)(2,1)}) fusion(bf16[8192,256]{0,1:T(8,128)(2,1)} %collective-permute-done.2, bf16[8192,256]{0,1:T(8,128)(2,1)} %convolution_convert_fusion.1, pred[]{:T(512)S(6)} %eq.65), kind=kLoop, calls=%fused_computation.15 | loop fusion | flops 4194304 | bytes 16777216 | tf_op jit(solution)/shard_map/jit(_where)/select_n | solution.py:90
  481.7 10.4 %fusion = f32[512,512]{1,0:T(8,128)S(1)} fusion(bf16[8192,256]{0,1:T(8,128)(2,1)} %get-tuple-element.14, bf16[8192,256]{0,1:T(8,128)(2,1)} %get-tuple-element.13), kind=kOutput, calls=%fused_computation.6 | convolution fusion | flops 4311744512 | bytes 9437184 | tf_op jit(solution)/shard_map/dot_general | solution.py:74
  493.4 20.1 %all_to_all.60 = f32[16,1,16384]{2,1,0:T(1,128)S(1)} all-to-all(f32[16,1,16384]{2,1,0:T(1,128)S(1)} %all_to_all.50), channel_id=1, replica_groups=mesh['space'=16,'group'=8] {'space'}, dimensions={0} | all-to-all | bytes 2097152 | tf_op jit(solution)/shard_map/all_to_all | solution.py:26
  514.1 1.8 broadcast_in_dim.18
  515.9 4.9 all-to-all-start.5
  520.8 15.9 %all-to-all-done.5 = f32[16,1,16384]{2,1,0:T(1,128)S(1)} async-done(((f32[16,1,16384]{2,1,0:T(1,128)}), f32[16,1,16384]{2,1,0:T(1,128)S(1)}, u32[]{:S(2)}, u32[]{:S(2)}) %all-to-all-start.5) | async-done | bytes 1048608 | tf_op jit(solution)/shard_map/all_to_all | solution.py:45
  540.4 6.9 %fusion.54 = (f32[16,16384]{1,0:T(8,128)S(1)}, f32[16,16384]{1,0:T(8,128)}) fusion(f32[]{:T(128)S(6)} %add.38, s32[16,1,16384]{2,1,0:T(1,128)S(1)} %iota.278, s32[16384]{0:T(1024)S(1)} %bitcast.106, f32[16,1,16384]{2,1,0:T(1,128)S(1)} %all-to-all-done.5, f32[]{:T(128)S(6)} %div.139), kind=kLoop, calls=%fused_computation.105 | loop fusion | flops 1310720 | bytes 4259848 | tf_op jit(solution)/shard_map/div | solution.py:62
  548.7 1.8 fusion.67
  550.7 1.9 fusion.7
  552.7 1.8 fusion.68
  554.5 1.9 fusion.6
  556.4 1.8 fusion.69
  558.2 1.9 fusion.5
  560.1 1.8 fusion.70
  562.0 2.1 fusion.4
  564.1 1.8 fusion.71
  566.0 1.9 fusion.3
  567.8 2.0 fusion.21
  569.9 2.7 convolution_convert_fusion
  (39 shorter events, 20.9 us)
Async XLA Ops:
  0.0 92.2 %collective-permute-start = (bf16[8192,256]{1,0:T(8,128)(2,1)}, bf16[8192,256]{1,0:T(8,128)(2,1)}, u32[]{:S(2)}, u32[]{:S(2)}) collective-permute-start(bf16[8192,256]{1,0:T(8,128)(2,1)} %param.2), channel_id=1, source_target_pairs={{0,1},{1,0},{2,3},{3,2},{4,5},{5,4},{6,7},{7,6},{8,9},{9,8},{10,11... | collective-permute-start | bytes 12582920 | tf_op jit(solution)/shard_map/ppermute | solution.py:16
  96.0 1.9 copy-start.2
  96.0 3.2 copy-start.4
  130.2 21.0 %all-to-all-start.1 = ((f32[16,1,16384]{2,1,0:T(1,128)}), f32[16,1,16384]{2,1,0:T(1,128)S(1)}, u32[]{:S(2)}, u32[]{:S(2)}) async-start(f32[16,1,16384]{2,1,0:T(1,128)} %broadcast_in_dim.15), calls=%async_computation.1 | async-start | bytes 2097152 | tf_op jit(solution)/shard_map/all_to_all | solution.py:45
  180.2 8.1 %copy-start.5 = (bf16[8192,256]{1,0:T(8,128)(2,1)S(1)}, bf16[8192,256]{1,0:T(8,128)(2,1)}, u32[]{:S(2)}) copy-start(bf16[8192,256]{1,0:T(8,128)(2,1)} %copy-done.4) | copy-start | bytes 12582916
  182.6 5.8 %copy-start.3 = (bf16[8192,256]{1,0:T(8,128)(2,1)S(1)}, bf16[8192,256]{1,0:T(8,128)(2,1)}, u32[]{:S(2)}) copy-start(bf16[8192,256]{1,0:T(8,128)(2,1)} %copy-done.2) | copy-start | bytes 12582916
  192.3 93.2 %collective-permute-start.1 = (bf16[8192,256]{0,1:T(8,128)(2,1)}, bf16[8192,256]{0,1:T(8,128)(2,1)}, u32[]{:S(2)}, u32[]{:S(2)}) collective-permute-start(bf16[8192,256]{0,1:T(8,128)(2,1)} %convolution_convert_fusion.2), channel_id=1, source_target_pairs={{0,2},{2,0},{1,3},{3,1},{4,6},{6,4},{5,7},{7,5},{8,10},{10,8},{9,1... | collective-permute-start | bytes 12582920 | tf_op jit(solution)/shard_map/ppermute | solution.py:16
  370.5 8.1 %copy-start.7 = (bf16[8192,256]{0,1:T(8,128)(2,1)S(1)}, bf16[8192,256]{0,1:T(8,128)(2,1)}, u32[]{:S(2)}) copy-start(bf16[8192,256]{0,1:T(8,128)(2,1)} %get-tuple-element.16) | copy-start | bytes 12582916
  372.8 5.8 %copy-start.6 = (bf16[8192,256]{0,1:T(8,128)(2,1)S(1)}, bf16[8192,256]{0,1:T(8,128)(2,1)}, u32[]{:S(2)}) copy-start(bf16[8192,256]{0,1:T(8,128)(2,1)} %get-tuple-element.15) | copy-start | bytes 12582916
  382.7 93.1 %collective-permute-start.2 = (bf16[8192,256]{0,1:T(8,128)(2,1)}, bf16[8192,256]{0,1:T(8,128)(2,1)}, u32[]{:S(2)}, u32[]{:S(2)}) collective-permute-start(bf16[8192,256]{0,1:T(8,128)(2,1)} %convolution_convert_fusion.1), channel_id=1, source_target_pairs={{0,4},{4,0},{1,5},{5,1},{2,6},{6,2},{3,7},{7,3},{8,12},{12,8},{9,1... | collective-permute-start | bytes 12582920 | tf_op jit(solution)/shard_map/ppermute | solution.py:16
  515.9 20.7 %all-to-all-start.5 = ((f32[16,1,16384]{2,1,0:T(1,128)}), f32[16,1,16384]{2,1,0:T(1,128)S(1)}, u32[]{:S(2)}, u32[]{:S(2)}) async-start(f32[16,1,16384]{2,1,0:T(1,128)} %broadcast_in_dim.18), calls=%async_computation.5 | async-start | bytes 2097152 | tf_op jit(solution)/shard_map/all_to_all | solution.py:45
  562.0 7.9 %copy-start.1 = (bf16[8192,256]{0,1:T(8,128)(2,1)S(1)}, bf16[8192,256]{0,1:T(8,128)(2,1)}, u32[]{:S(2)}) copy-start(bf16[8192,256]{0,1:T(8,128)(2,1)} %get-tuple-element.14) | copy-start | bytes 12582916
  564.1 5.8 %copy-start = (bf16[8192,256]{0,1:T(8,128)(2,1)S(1)}, bf16[8192,256]{0,1:T(8,128)(2,1)}, u32[]{:S(2)}) copy-start(bf16[8192,256]{0,1:T(8,128)(2,1)} %get-tuple-element.13) | copy-start | bytes 12582916
where the time goes:
time: 580 us; the launch traced here: 574 us
  waiting for transfers between devices  299 us (52%)
  matrix products  104 us (18%)
  blocking collectives  81.1 us (14%)
  other arithmetic  47 us (8%)
  local copies, waits for them, and re-layouts  20.1 us (3%)
  starting transfers between devices  18.1 us (3%)
    ppermute x3, waiting for transfers between devices, from_partner(): return lax.ppermute(block, axis, route)  270 us
    all_to_all x3, blocking collectives, summed_on_arrival(): lax.all_to_all(pieces, axis, split_axis=0, concat_axis=0, tiled=True)  62 us
    dot_general x15, matrix products, filter_mix(): cube = jnp.dot(square, iterate, precision=lax.Precision.HIGHEST)  31.7 us
    dot_general x15, matrix products, filter_mix(): square = jnp.dot(iterate, iterate, precision=lax.Precision.HIGHEST)  29.7 us
    all_to_all x2, waiting for transfers between devices, sent_to_all(): return lax.all_to_all(copies, axis, split_axis=0, concat_axis=0, tiled=True)  28.6 us
    dot_general x3, matrix products, local_gram(): lax.dot_general(stacked, stacked, (((0,), (0,)), ((), ())), preferred_ele...  25.2 us
    div x3, other arithmetic, filter_mix(): scaled = gram / (jnp.trace(gram) / width)  20.8 us
    all_to_all x1, blocking collectives, sent_to_all(): return lax.all_to_all(copies, axis, split_axis=0, concat_axis=0, tiled=True)  19.1 us
  transfers between devices with their start and end apart: 5, of which 5 were waited for; matrix products, arithmetic and copies ran while one was open for 1% of the time, Pallas kernels for 0%

commit v1 on v0

v1 whole, which is shorter than its diff:
```python
import functools

import jax
import jax.numpy as jnp
from jax import lax
from jax.experimental import pallas as pl
from jax.experimental.pallas import tpu as pltpu
from jax.sharding import PartitionSpec as P

STEPS = 5
MESH = pl.DeviceIdType.MESH
F32 = jnp.float32
BF16 = jnp.bfloat16
CHUNKS = 8
ORDER = ((2, 1), (1, 1), (3, 1), (0, 1), (2, 0), (1, 0), (3, 0))


def dot(a, b):
    return jnp.dot(a, b, preferred_element_type=F32)


def dot_t(a, b):
    return lax.dot_general(a, b, (((0,), (0,)), ((), ())), preferred_element_type=F32)


def split(a):
    high = a.astype(BF16)
    return high, (a - high.astype(F32)).astype(BF16)


def loop(low, high, body):
    def step(i, carry):
        body(i)
        return carry

    lax.fori_loop(low, high, step, 0)


def start_of_filter(gram):
    width = gram.shape[0]
    row = lax.broadcasted_iota(jnp.int32, gram.shape, 0)
    col = lax.broadcasted_iota(jnp.int32, gram.shape, 1)
    eye = row == col
    trace = jnp.sum(jnp.where(eye, gram, 0.0), axis=(0, 1), keepdims=True)
    shifted = gram * (1.0 / (trace / width)) - jnp.where(eye, 1.0, 0.0)
    norm = jnp.sqrt(jnp.sum(shifted * shifted, axis=(0, 1), keepdims=True))
    return shifted * (1.0 / (1.0 + norm))


def filter_step(iterate):
    low = iterate.astype(BF16)
    square = dot(low, low).astype(BF16)
    return 1.5 * iterate - 0.5 * dot(square, low)


def mix_of(iterate, sketch):
    return (0.5 * (sketch + dot(iterate.astype(BF16), sketch.astype(BF16)))).astype(BF16)


def projected(gram, mix):
    high, low = split(gram)
    half = dot(high, mix) + dot(low, mix)
    high, low = split(half)
    return dot_t(mix, high) + dot_t(mix, low)


def kernel(
    n_space, n_group,
    x_hbm, sk_hbm, out_ref,
    panels, own, sketch, diag, diag_in, diag_all,
    cs0, cr0, cg0, ca0, cs1, cr1, cg1, ca1, cs2, cr2, cg2, ca2,
    gram0, gram1, gram2, it0, it1, mix0, mix1, p1, p2, block2,
    a_send, a_recv, l_sem, dr_send, dr_recv, dg_send, dg_recv, da_send, da_recv,
    r_send, r_recv, g_send, g_recv, k_send, k_recv, c_send, c_recv,
):
    s = lax.axis_index("space")
    g = lax.axis_index("group")
    width = x_hbm.shape[1]
    block = x_hbm.shape[0] // n_group
    n_k = n_space // 2
    k = lax.div(s, 2)
    c = lax.rem(s, 2)
    gx = lax.rem(g, 4)
    gz = lax.div(g, 4)
    part = width // n_k
    partner = 2 * k + 1 - c

    def remote(src, dst, send, recv, to):
        return pltpu.make_async_remote_copy(
            src_ref=src, dst_ref=dst, send_sem=send, recv_sem=recv,
            device_id=to, device_id_type=MESH,
        )

    def group_peer(d):
        return s, lax.rem(g + d, n_group)

    def space_peer(d):
        return lax.rem(s + d, n_space), g

    def core_peer(d):
        return 2 * lax.rem(k + d, n_k) + c, g

    barrier = pltpu.get_barrier_semaphore()
    loop(1, n_group, lambda d: pl.semaphore_signal(
        barrier, inc=1, device_id=group_peer(d), device_id_type=MESH))
    loop(1, n_space, lambda d: pl.semaphore_signal(
        barrier, inc=1, device_id=space_peer(d), device_id_type=MESH))

    whole = pltpu.make_async_copy(x_hbm, own, l_sem.at[0])
    whole.start()
    mine = pltpu.make_async_copy(
        x_hbm.at[pl.ds(pl.multiple_of(g * block, block), block)], panels.at[g], l_sem.at[1])
    mine.start()
    tests = pltpu.make_async_copy(sk_hbm, sketch, l_sem.at[2])
    tests.start()
    pl.semaphore_wait(barrier, n_group - 1 + n_space - 1)

    piece = block // CHUNKS

    def panel_copy(i, at, size):
        dx, dz = ORDER[i]
        to = lax.rem(gz + dz, 2) * 4 + lax.rem(gx + dx, 4)
        return remote(
            x_hbm.at[pl.ds(pl.multiple_of(to * block + at, size), size)],
            panels.at[g, pl.ds(pl.multiple_of(at, size), size)],
            a_send.at[i], a_recv.at[i], (s, to))

    def send_pieces(ch):
        for i in range(len(ORDER)):
            panel_copy(i, ch * piece, piece).start()

    loop(0, CHUNKS // 2, send_pieces)

    whole.wait()
    diag[...] = jnp.zeros_like(diag)

    def add_diag(j):
        rows = own[pl.ds(pl.multiple_of(j * block, block), block), :]
        diag[...] += dot_t(rows, rows)

    loop(0, n_group, add_diag)

    def diag_copy(d):
        to = lax.rem(k + d, n_k)
        return remote(
            diag.at[pl.ds(pl.multiple_of(to * part, part), part)], diag_in.at[s],
            dr_send.at[d], dr_recv.at[s], (2 * to + gz, g))

    keeps = c == gz
    loop(1, n_k, lambda d: diag_copy(d).start())

    @pl.when(jnp.logical_not(keeps))
    def _():
        diag_copy(0).start()

    @pl.when(keeps)
    def _():
        diag_in[s] = diag[pl.ds(pl.multiple_of(k * part, part), part), :]

        def arrived(d):
            at = lax.rem(s + d, n_space)
            remote(diag.at[pl.ds(0, part)], diag_in.at[at], dr_send.at[0], dr_recv.at[at],
                   (at, g)).wait_recv()

        loop(1, n_space, arrived)
        diag_all[k, gx] = jnp.sum(diag_in[...], axis=0)

        def pass_on(d):
            remote(diag_all.at[k, gx], diag_all.at[k, gx], dg_send.at[d], dg_recv.at[gx],
                   group_peer(d)).start()

        loop(1, n_group, pass_on)

    loop(CHUNKS // 2, CHUNKS, send_pieces)

    def diag_arrived(j):
        @pl.when(4 * c + j != g)
        def _():
            remote(diag_all.at[k, j], diag_all.at[k, j], dg_send.at[0], dg_recv.at[j],
                   (s, 4 * c + j)).wait_recv()

    loop(0, 4, diag_arrived)

    def diag_gather(d):
        return remote(diag_all.at[k], diag_all.at[k], da_send.at[d], da_recv.at[d], core_peer(d))

    loop(1, n_k, lambda d: diag_gather(d).start())

    def reduce_cross(level, cs, cr, cg, ca, everyone, beside):
        def scatter(d):
            to = lax.rem(s + d, n_space)
            return remote(cs.at[to], cr.at[s], r_send.at[level, d], r_recv.at[level, d], (to, g))

        def share(d):
            return remote(cg.at[g], cg.at[g], g_send.at[level, d], g_recv.at[level, d],
                          group_peer(d))

        at = s if everyone else k
        peers = n_space if everyone else n_k

        def gather(d):
            return remote(ca.at[at], ca.at[at], k_send.at[level, d], k_recv.at[level, d],
                          space_peer(d) if everyone else core_peer(d))

        loop(1, n_space, lambda d: scatter(d).start())
        cr[s] = cs[s]
        beside()
        loop(1, n_space, lambda d: scatter(d).wait_recv())
        cg[g] = jnp.sum(cr[...].astype(F32), axis=0).astype(BF16)
        loop(1, n_group, lambda d: share(d).start())
        loop(1, n_group, lambda d: share(d).wait_recv())
        ca[at] = jnp.sum(cg[...].astype(F32), axis=0).astype(BF16)
        loop(1, peers, lambda d: gather(d).start())
        loop(1, peers, lambda d: gather(d).wait_recv())

        def sent():
            loop(1, n_space, lambda d: scatter(d).wait_send())
            loop(1, n_group, lambda d: share(d).wait_send())
            loop(1, peers, lambda d: gather(d).wait_send())

        return sent

    def apply_mix(src, a, b, mix, dst, at):
        upper, lower = mix[:width, :], mix[width:, :]
        tile = 256

        def rows(j):
            here = pl.ds(pl.multiple_of(j * tile, tile), tile)
            dst[at, here, :] = (dot(src[a, here, :], upper) + dot(src[b, here, :], lower)).astype(BF16)

        loop(0, block // tile, rows)

    def fill(gram, at, cross):
        gram[at, :width, width:] = cross
        gram[at, width:, :width] = cross.T

    mine.wait()
    for i in range(len(ORDER)):
        panel_copy(i, 0, block).wait_recv()
    for p in range(4):
        cross = dot_t(panels[2 * p], panels[2 * p + 1]).astype(BF16).reshape(n_k, part, width)
        for kk in range(n_k):
            cs0[2 * kk + p // 2, p % 2] = cross[kk]

    def beside0():
        loop(1, n_k, lambda d: diag_gather(d).wait_recv())
        for i in range(2):
            gram0[i, :width, :width] = diag_all[:, 2 * i].reshape(width, width)
            gram0[i, width:, width:] = diag_all[:, 2 * i + 1].reshape(width, width)

    sent0 = reduce_cross(0, cs0, cr0, cg0, ca0, False, beside0)
    for i in range(2):
        fill(gram0, i, ca0[:, i].astype(F32).reshape(width, width))
        it0[i] = start_of_filter(gram0[i])

    def steps0(_):
        for i in range(2):
            it0[i] = filter_step(it0[i])

    loop(0, STEPS, steps0)
    tests.wait()
    for i in range(2):
        mix0[2 * c + i] = mix_of(it0[i], sketch[0])
    swap0 = remote(mix0.at[pl.ds(2 * c, 2)], mix0.at[pl.ds(2 * c, 2)], c_send.at[0], c_recv.at[0],
                   (partner, g))
    swap0.start()

    for i in range(2):
        pair = 2 * c + i
        apply_mix(panels, 2 * pair, 2 * pair + 1, mix0[pair], p1, pair)
    swap0.wait_recv()
    for i in range(2):
        pair = 2 * (1 - c) + i
        apply_mix(panels, 2 * pair, 2 * pair + 1, mix0[pair], p1, pair)
    for q in range(2):
        cross = dot_t(p1[2 * q], p1[2 * q + 1]).astype(BF16).reshape(n_k, part, width)
        for kk in range(n_k):
            cs1[2 * kk + q] = cross[kk]

    def beside1():
        gram1[0, :width, :width] = projected(gram0[0], mix0[2 * c])
        gram1[0, width:, width:] = projected(gram0[1], mix0[2 * c + 1])

    sent1 = reduce_cross(1, cs1, cr1, cg1, ca1, False, beside1)
    fill(gram1, 0, ca1[...].astype(F32).reshape(width, width))
    it1[...] = start_of_filter(gram1[0])

    def steps1(_):
        it1[...] = filter_step(it1[...])

    loop(0, STEPS, steps1)
    mix1[c] = mix_of(it1[...], sketch[1])
    swap1 = remote(mix1.at[c], mix1.at[c], c_send.at[1], c_recv.at[1], (partner, g))
    swap1.start()

    apply_mix(p1, 2 * c, 2 * c + 1, mix1[c], p2, c)
    swap1.wait_recv()
    apply_mix(p1, 2 * (1 - c), 2 * (1 - c) + 1, mix1[1 - c], p2, 1 - c)
    cross = dot_t(p2[0], p2[1]).astype(BF16).reshape(n_space, width // n_space, width)
    cs2[...] = cross
    swap2 = remote(block2.at[c], block2.at[c], c_send.at[2], c_recv.at[2], (partner, g))

    def beside2():
        block2[c] = projected(gram1[0], mix1[c])
        swap2.start()

    sent2 = reduce_cross(2, cs2, cr2, cg2, ca2, True, beside2)
    swap2.wait_recv()
    gram2[0, :width, :width] = block2[0]
    gram2[0, width:, width:] = block2[1]
    fill(gram2, 0, ca2[...].astype(F32).reshape(width, width))
    it1[...] = start_of_filter(gram2[0])
    loop(0, STEPS, steps1)
    last = mix_of(it1[...], sketch[2])
    upper, lower = last[:width, :], last[width:, :]
    tile = 256

    def rows(j):
        here = pl.ds(pl.multiple_of(j * tile, tile), tile)
        out_ref[here, :] = (dot(p2[0, here, :], upper) + dot(p2[1, here, :], lower)).astype(BF16)

    loop(0, block // tile, rows)

    for i in range(len(ORDER)):
        panel_copy(i, 0, block).wait_send()
    loop(1, n_k, lambda d: diag_copy(d).wait_send())

    @pl.when(jnp.logical_not(keeps))
    def _():
        diag_copy(0).wait_send()

    @pl.when(keeps)
    def _():
        loop(1, n_group, lambda d: remote(
            diag_all.at[k, gx], diag_all.at[k, gx], dg_send.at[d], dg_recv.at[gx],
            group_peer(d)).wait_send())

    loop(1, n_k, lambda d: diag_gather(d).wait_send())
    sent0()
    sent1()
    sent2()
    for swap in (swap0, swap1, swap2):
        swap.wait_send()


def body(n_space, n_group, snapshot_basis, sketch):
    rows, width = snapshot_basis.shape
    block = rows // n_group
    n_k = n_space // 2
    part = width // n_k
    dma = pltpu.SemaphoreType.DMA
    vmem = pltpu.VMEM
    scratch = [
        vmem((n_group, block, width), BF16), vmem((rows, width), BF16), vmem(sketch.shape, F32),
        vmem((width, width), F32), vmem((n_space, part, width), F32), vmem((n_k, 4, part, width), F32),
        vmem((n_space, 2, part, width), BF16), vmem((n_space, 2, part, width), BF16),
        vmem((n_group, 2, part, width), BF16), vmem((n_k, 2, part, width), BF16),
        vmem((n_space, part, width), BF16), vmem((n_space, part, width), BF16),
        vmem((n_group, part, width), BF16), vmem((n_k, part, width), BF16),
        vmem((n_space, part // 2, width), BF16), vmem((n_space, part // 2, width), BF16),
        vmem((n_group, part // 2, width), BF16), vmem((n_space, part // 2, width), BF16),
        vmem((2, 2 * width, 2 * width), F32), vmem((1, 2 * width, 2 * width), F32),
        vmem((1, 2 * width, 2 * width), F32),
        vmem((2, 2 * width, 2 * width), F32), vmem((2 * width, 2 * width), F32),
        vmem((4, 2 * width, width), BF16), vmem((2, 2 * width, width), BF16),
        vmem((4, block, width), BF16), vmem((2, block, width), BF16), vmem((2, width, width), F32),
        dma((len(ORDER),)), dma((len(ORDER),)), dma((3,)),
        dma((n_k,)), dma((n_space,)), dma((n_group,)), dma((4,)), dma((n_k,)), dma((n_k,)),
        dma((3, n_space)), dma((3, n_space)), dma((3, n_group)), dma((3, n_group)),
        dma((3, n_space)), dma((3, n_space)), dma((3,)), dma((3,)),
    ]
    return pl.pallas_call(
        functools.partial(kernel, n_space, n_group),
        out_shape=jax.ShapeDtypeStruct((block, width), BF16),
        in_specs=[pl.BlockSpec(memory_space=pl.ANY)] * 2,
        out_specs=pl.BlockSpec(memory_space=pltpu.VMEM),
        scratch_shapes=scratch,
        compiler_params=pltpu.CompilerParams(
            collective_id=0, has_side_effects=True, vmem_limit_bytes=56 * 1024 * 1024),
        name="merge",
    )(snapshot_basis, sketch)


def solution(mesh):
    in_specs = (P("space", "group"), P())
    out_specs = P(("space", "group"), None)
    step = functools.partial(body, mesh.shape["space"], mesh.shape["group"])
    return jax.shard_map(step, mesh=mesh, in_specs=in_specs, out_specs=out_specs, check_vma=False)
```

time: 580 us -> 151 us (0.26); the launches traced: 574 us -> 151 us
  waiting for transfers between devices: 299 us -> 0 us
  Pallas kernels: 0 us -> 149 us
  matrix products: 104 us -> 0 us
  blocking collectives: 81.1 us -> 0 us
  other arithmetic: 47 us -> 0 us
  local copies, waits for them, and re-layouts: 20.1 us -> 1.87 us
  starting transfers between devices: 18.1 us -> 0 us
    ppermute x3 -> x0, waiting for transfers between devices: 270 us -> none  [from_partner(): return lax.ppermute(block, axis, route)]
    pallas_call x0 -> x1, Pallas kernels: none -> 149 us  [body(): pl.pallas_call(functools.partial(kernel, n_space, n_group), out_shape=jax...]
    dot_general x39 -> x0, matrix products: 104 us -> none  [the longest x15 31.7 us: filter_mix(): cube = jnp.dot(square, iterate, precision=lax.Precision.HIGHEST)]
    all_to_all x4 -> x0, blocking collectives: 81.1 us -> none  [the longest x3 62 us: summed_on_arrival(): lax.all_to_all(pieces, axis, split_axis=0, concat_axis=0, tiled=True)]
    all_to_all x2 -> x0, waiting for transfers between devices: 28.6 us -> none  [sent_to_all(): return lax.all_to_all(copies, axis, split_axis=0, concat_axis=0, tiled=True)]
    div x3 -> x0, other arithmetic: 20.8 us -> none  [filter_mix(): scaled = gram / (jnp.trace(gram) / width)]
    select_n x3 -> x0, other arithmetic: 15.6 us -> none  [body(): lower_part = jnp.where(upper, other, own_panel)]
    reduce_sum x9 -> x0, other arithmetic: 10.5 us -> none  [the longest x3 4.96 us: filter_mix(): scaled = gram / (jnp.trace(gram) / width)]
  transfers between devices with their start and end apart: 5 -> 0, of which waited for: 5 -> 0; matrix products, arithmetic and copies ran while one was open for 1% -> 0% of each run, Pallas kernels for 0% -> 0%
where the time goes in v1:
time: 151 us
  Pallas kernels  149 us (99%)
  local copies, waits for them, and re-layouts  1.87 us (1%)
    pallas_call x1, Pallas kernels, body(): pl.pallas_call(functools.partial(kernel, n_space, n_group), out_shape=jax...  149 us

profile of v1, /device:TPU:1, one launch (start us, length us, event | category | flops | bytes accessed | tf_op | source)
XLA Modules:
  0.0 151.1 jit_solution(6963365592451737062)
XLA Ops:
  0.0 149.2 %merge.1 = bf16[1024,256]{1,0:T(8,128)(2,1)} custom-call(bf16[8192,256]{1,0:T(8,128)(2,1)} %x_hbm.1, f32[3,512,256]{2,1,0:T(8,128)} %sk_hbm.1), custom_call_target="tpu_custom_call" | custom-call | tf_op jit(solution)/shard_map/merge/pallas_call | solution.py:372
  149.2 1.9 %copy.4 = bf16[1024,256]{1,0:T(8,128)(2,1)} copy(bf16[1024,256]{1,0:T(8,128)(2,1)} %merge.1) | data formatting | bytes 1048576

commit v2 on v1

v2 whole, which is shorter than its diff:
```python
import functools

import jax
import jax.numpy as jnp
from jax import lax
from jax.experimental import pallas as pl
from jax.experimental.pallas import tpu as pltpu
from jax.sharding import PartitionSpec as P

STEPS = 5
MESH = pl.DeviceIdType.MESH
F32 = jnp.float32
BF16 = jnp.bfloat16
SPAN = 4
PIECES = 4
SPLIT = 2


def dot(a, b):
    return jnp.dot(a, b, preferred_element_type=F32)


def dot_t(a, b):
    return lax.dot_general(a, b, (((0,), (0,)), ((), ())), preferred_element_type=F32)


def split(a):
    high = a.astype(BF16)
    return high, (a - high.astype(F32)).astype(BF16)


def loop(low, high, body):
    def step(i, carry):
        body(i)
        return carry

    lax.fori_loop(low, high, step, 0)


def start_of_filter(gram):
    width = gram.shape[0]
    row = lax.broadcasted_iota(jnp.int32, gram.shape, 0)
    col = lax.broadcasted_iota(jnp.int32, gram.shape, 1)
    eye = row == col
    trace = jnp.sum(jnp.where(eye, gram, 0.0), axis=(0, 1), keepdims=True)
    shifted = gram * (1.0 / (trace / width)) - jnp.where(eye, 1.0, 0.0)
    norm = jnp.sqrt(jnp.sum(shifted * shifted, axis=(0, 1), keepdims=True))
    return shifted * (1.0 / (1.0 + norm))


def filter_step(iterate):
    low = iterate.astype(BF16)
    square = dot(low, low).astype(BF16)
    return 1.5 * iterate - 0.5 * dot(square, low)


def mix_of(iterate, sketch):
    return (0.5 * (sketch + dot(iterate.astype(BF16), sketch.astype(BF16)))).astype(BF16)


def projected(gram, mix):
    high, low = split(gram)
    half = dot(high, mix) + dot(low, mix)
    high, low = split(half)
    return dot_t(mix, high) + dot_t(mix, low)


def kernel(
    n_space, n_group,
    x_hbm, sk_hbm, out_ref,
    panels, other, own, sketch, diag, diag_in, diag_all,
    cs0, cr0, cg0, ca0, cs1, cr1, cg1, ca1, cs2, cr2, cg2, ca2,
    gram, gram1, it, mix0, mix1, p1, po, q, block1, block2,
    a_send, a_recv, b_send, b_recv, f_send, f_recv, l_sem,
    dr_send, dr_recv, dg_send, dg_recv, da_send, da_recv,
    r_send, r_recv, g_send, g_recv, k_send, k_recv, c_send, c_recv, z_send, z_recv,
):
    s = lax.axis_index("space")
    g = lax.axis_index("group")
    width = x_hbm.shape[1]
    block = x_hbm.shape[0] // n_group
    n_k = n_space // 2
    k = lax.div(s, 2)
    c = lax.rem(s, 2)
    gx = lax.rem(g, SPAN)
    gz = lax.div(g, SPAN)
    far = 1 - gz
    part = width // n_k
    half = width
    partner = (2 * k + 1 - c, g)

    def remote(src, dst, send, recv, to):
        return pltpu.make_async_remote_copy(
            src_ref=src, dst_ref=dst, send_sem=send, recv_sem=recv,
            device_id=to, device_id_type=MESH,
        )

    def group_peer(d):
        return s, lax.rem(g + d, n_group)

    def x_peer(d):
        return s, gz * SPAN + lax.rem(gx + d, SPAN)

    def space_peer(d):
        return lax.rem(s + d, n_space), g

    def core_peer(d):
        return 2 * lax.rem(k + d, n_k) + c, g

    def z_peer(core):
        return lax.rem(s - c + n_space // 2, n_space) + core, far * SPAN + gx

    closing = []

    def finish():
        for close in closing:
            close()

    barrier = pltpu.get_barrier_semaphore()

    def greet(to):
        pl.semaphore_signal(barrier, inc=1, device_id=to, device_id_type=MESH)

    loop(1, n_group, lambda d: greet(group_peer(d)))
    loop(1, n_space, lambda d: greet(space_peer(d)))
    loop(0, 2, lambda core: greet(z_peer(core)))

    whole = pltpu.make_async_copy(x_hbm, own, l_sem.at[0])
    whole.start()

    def block_rows(h, x):
        return pl.ds(pl.multiple_of((h * SPAN + x) * block, block), block)

    def mine(h):
        return pltpu.make_async_copy(x_hbm.at[block_rows(h, gx)], panels.at[h, gx], l_sem.at[1 + h])

    mine(0).start()
    mine(1).start()
    tests = pltpu.make_async_copy(sk_hbm, sketch, l_sem.at[3])
    tests.start()
    pl.semaphore_wait(barrier, n_group - 1 + n_space - 1 + 2)

    piece = block // PIECES

    def x_copy(d, h, at, size, send, recv):
        to = lax.rem(gx + d, SPAN)
        return remote(
            x_hbm.at[pl.ds(pl.multiple_of((h * SPAN + to) * block + at, size), size)],
            panels.at[h, gx, pl.ds(pl.multiple_of(at, size), size)],
            send, recv, (s, gz * SPAN + to))

    def first(d, p):
        return x_copy(d, far, p * piece, piece, a_send.at[d - 1, p], a_recv.at[d - 1, p])

    def second(d):
        return x_copy(d, gz, 0, block, b_send.at[d - 1], b_recv.at[d - 1])

    def send_first(j):
        p = lax.div(j, SPLIT)
        for d in (2, 1, 3):
            x_copy(d, far, j * (piece // SPLIT), piece // SPLIT,
                   a_send.at[d - 1, p], a_recv.at[d - 1, p]).start()

    def send_second(j):
        for d in (2, 1, 3):
            x_copy(d, gz, j * (piece // SPLIT), piece // SPLIT,
                   b_send.at[d - 1], b_recv.at[d - 1]).start()

    loop(0, PIECES * SPLIT, send_first)

    @closing.append
    def _():
        for d in (1, 2, 3):
            loop(0, PIECES, lambda p: first(d, p).wait_send())
            second(d).wait_send()

    def pass_rows(d, at, size):
        x = lax.rem(gx - d + SPAN, SPAN)
        rows = pl.ds(pl.multiple_of(at, size), size)
        return remote(panels.at[far, x, rows], other.at[x, rows], f_send.at[d], f_recv.at[d],
                      (s, far * SPAN + gx))

    def pass_piece(p):
        for d in (2, 1, 3):
            first(d, p).wait_recv()
            pass_rows(d, p * piece, piece).start()

    @closing.append
    def _():
        for d in range(SPAN):
            pass_rows(d, 0, block).wait_send()

    whole.wait()
    diag[...] = jnp.zeros_like(diag)

    def add_diag(j):
        rows = own[pl.ds(pl.multiple_of(j * block, block), block), :]
        diag[...] += dot_t(rows, rows)

    loop(0, n_group, add_diag)
    owner = lax.div(gx, 2)
    slot = lax.rem(gx, 2)

    def diag_copy(d):
        to = lax.rem(k + d, n_k)
        return remote(
            diag.at[pl.ds(pl.multiple_of(to * part, part), part)], diag_in.at[s],
            dr_send.at[d], dr_recv.at[s], (2 * to + owner, g))

    keeps = c == owner
    loop(1, n_k, lambda d: diag_copy(d).start())
    closing.append(lambda: loop(1, n_k, lambda d: diag_copy(d).wait_send()))

    @pl.when(jnp.logical_not(keeps))
    def _():
        diag_copy(0).start()

    mine(0).wait()
    mine(1).wait()
    pass_rows(0, 0, block).start()

    def pass_diag(d):
        return remote(diag_all.at[k, slot], diag_all.at[k, slot], dg_send.at[d], dg_recv.at[slot],
                      x_peer(d))

    @pl.when(keeps)
    def _():
        diag_in[s] = diag[pl.ds(pl.multiple_of(k * part, part), part), :]

        def arrived(d):
            at = lax.rem(s + d, n_space)
            remote(diag.at[pl.ds(0, part)], diag_in.at[at], dr_send.at[0], dr_recv.at[at],
                   (at, g)).wait_recv()

        loop(1, n_space, arrived)
        diag_all[k, slot] = jnp.sum(diag_in[...], axis=0)
        loop(1, SPAN, lambda d: pass_diag(d).start())

    @closing.append
    def _():
        @pl.when(jnp.logical_not(keeps))
        def _():
            diag_copy(0).wait_send()

        @pl.when(keeps)
        def _():
            loop(1, SPAN, lambda d: pass_diag(d).wait_send())

    loop(0, PIECES * SPLIT, send_second)
    loop(0, PIECES - 1, pass_piece)

    def diag_arrived(j):
        @pl.when(2 * c + j != gx)
        def _():
            remote(diag_all.at[k, j], diag_all.at[k, j], dg_send.at[0], dg_recv.at[j],
                   (s, gz * SPAN + 2 * c + j)).wait_recv()

    loop(0, 2, diag_arrived)

    def diag_gather(d):
        return remote(diag_all.at[k], diag_all.at[k], da_send.at[d], da_recv.at[d], core_peer(d))

    loop(1, n_k, lambda d: diag_gather(d).start())
    closing.append(lambda: loop(1, n_k, lambda d: diag_gather(d).wait_send()))

    def reduce_cross(level, cs, cr, cg, ca, all_groups, everyone, beside):
        mid, mids, mid_peer = (g, n_group, group_peer) if all_groups else (gx, SPAN, x_peer)
        at, peers, peer = (s, n_space, space_peer) if everyone else (k, n_k, core_peer)

        def scatter(d):
            to = lax.rem(s + d, n_space)
            return remote(cs.at[to], cr.at[s], r_send.at[level, d], r_recv.at[level, d], (to, g))

        def share(d):
            return remote(cg.at[mid], cg.at[mid], g_send.at[level, d], g_recv.at[level, d], mid_peer(d))

        def gather(d):
            return remote(ca.at[at], ca.at[at], k_send.at[level, d], k_recv.at[level, d], peer(d))

        loop(1, n_space, lambda d: scatter(d).start())
        cr[s] = cs[s]
        beside[0]()
        loop(1, n_space, lambda d: scatter(d).wait_recv())
        cg[mid] = jnp.sum(cr[...].astype(F32), axis=0).astype(BF16)
        loop(1, mids, lambda d: share(d).start())
        beside[1]()
        loop(1, mids, lambda d: share(d).wait_recv())
        ca[at] = jnp.sum(cg[...].astype(F32), axis=0).astype(BF16)
        loop(1, peers, lambda d: gather(d).start())
        beside[2]()
        loop(1, peers, lambda d: gather(d).wait_recv())

        @closing.append
        def _():
            loop(1, n_space, lambda d: scatter(d).wait_send())
            loop(1, mids, lambda d: share(d).wait_send())
            loop(1, peers, lambda d: gather(d).wait_send())

    tile = 256

    def mixed(a, b, mix, dst):
        upper, lower = mix[:width, :], mix[width:, :]

        def rows(j):
            here = pl.ds(pl.multiple_of(j * tile, tile), tile)
            dst[here, :] = (dot(a[here, :], upper) + dot(b[here, :], lower)).astype(BF16)

        loop(0, block // tile, rows)

    def filtered(upper, cross, lower, test, into):
        into[:width, :width] = upper
        into[width:, width:] = lower
        into[:width, width:] = cross
        into[width:, :width] = cross.T
        it[...] = start_of_filter(into[...])

        def step(_):
            it[...] = filter_step(it[...])

        loop(0, STEPS, step)
        return mix_of(it[...], test)

    def nothing():
        pass

    for d in (1, 2, 3):
        second(d).wait_recv()
    first_last = PIECES - 1
    for d in (1, 2, 3):
        first(d, first_last).wait_recv()
    for i in range(2):
        cross = dot_t(panels[0, 2 * i], panels[0, 2 * i + 1]) + dot_t(panels[1, 2 * i], panels[1, 2 * i + 1])
        cross = cross.astype(BF16).reshape(n_k, part, width)
        for kk in range(n_k):
            cs0[2 * kk + i] = cross[kk]

    def pass_last():
        for d in (2, 1, 3):
            pass_rows(d, first_last * piece, piece).start()

    reduce_cross(0, cs0, cr0, cg0, ca0, False, False, (
        pass_last, lambda: loop(1, n_k, lambda d: diag_gather(d).wait_recv()), nothing))
    tests.wait()
    mix0[0, c] = filtered(
        diag_all[:, 0].reshape(width, width), ca0[...].astype(F32).reshape(width, width),
        diag_all[:, 1].reshape(width, width), sketch[0], gram)
    swap0 = remote(mix0.at[0, c], mix0.at[0, c], c_send.at[0], c_recv.at[0], partner)
    swap0.start()
    closing.append(swap0.wait_send)

    def cross_z(n, src, dst):
        def copy(core):
            return remote(src, dst, z_send.at[n, core], z_recv.at[n, c], z_peer(core))

        def arrived(core, into):
            return remote(into, into, z_send.at[n, 0], z_recv.at[n, core], z_peer(core))

        loop(0, 2, lambda core: copy(core).start())
        closing.append(lambda: loop(0, 2, lambda core: copy(core).wait_send()))
        return arrived

    mixes = cross_z(0, mix0.at[0, c], mix0.at[1, c])

    def first_merge(pair):
        for h in range(2):
            mixed(panels.at[h, 2 * pair], panels.at[h, 2 * pair + 1], mix0.at[0, pair], p1.at[h, pair])

    first_merge(c)
    swap0.wait_recv()
    first_merge(1 - c)
    cross = dot_t(p1[0, 0], p1[0, 1]) + dot_t(p1[1, 0], p1[1, 1])
    cs1[...] = cross.astype(BF16).reshape(n_space, part // 2, width)
    swap1 = remote(block1.at[c], block1.at[c], c_send.at[1], c_recv.at[1], partner)

    def diag1():
        block1[c] = projected(gram[...], mix0[0, c])
        swap1.start()

    def other_rows():
        for core in range(2):
            mixes(core, mix0.at[1, core]).wait_recv()
        for d in range(SPAN):
            pass_rows(d, 0, block).wait_recv()
        for pair in range(2):
            mixed(other.at[2 * pair], other.at[2 * pair + 1], mix0.at[1, pair], po.at[pair])

    reduce_cross(1, cs1, cr1, cg1, ca1, False, True, (diag1, nothing, other_rows))
    swap1.wait_recv()
    closing.append(swap1.wait_send)
    mix1[0] = filtered(
        block1[0], ca1[...].astype(F32).reshape(width, width), block1[1], sketch[1], gram1)
    mine_half = pl.ds(pl.multiple_of(c * half, half), half)
    merges = cross_z(1, mix1.at[0, mine_half], mix1.at[1, mine_half])

    mixed(p1.at[gz, 0], p1.at[gz, 1], mix1.at[0], q.at[gz])
    for core in range(2):
        merges(core, mix1.at[1, pl.ds(core * half, half)]).wait_recv()
    mixed(po.at[0], po.at[1], mix1.at[1], q.at[far])
    cs2[...] = dot_t(q[0], q[1]).astype(BF16).reshape(n_space, part // 2, width)
    rows2 = pl.ds(pl.multiple_of(c * (width // 2), width // 2), width // 2)
    later = []

    def diag2():
        block2[gz] = projected(gram1[...], mix1[0])
        later.append(cross_z(2, block2.at[gz, rows2], block2.at[gz, rows2]))

    reduce_cross(2, cs2, cr2, cg2, ca2, True, True, (diag2, nothing, nothing))
    for core in range(2):
        later[0](core, block2.at[far, pl.ds(core * (width // 2), width // 2)]).wait_recv()
    last = filtered(
        block2[0], ca2[...].astype(F32).reshape(width, width), block2[1], sketch[2], gram)
    upper, lower = last[:width, :], last[width:, :]

    def rows(j):
        here = pl.ds(pl.multiple_of(j * tile, tile), tile)
        out_ref[here, :] = (dot(q[0, here, :], upper) + dot(q[1, here, :], lower)).astype(BF16)

    loop(0, block // tile, rows)
    finish()


def body(n_space, n_group, snapshot_basis, sketch):
    rows, width = snapshot_basis.shape
    block = rows // n_group
    n_k = n_space // 2
    part = width // n_k
    dma = pltpu.SemaphoreType.DMA
    vmem = pltpu.VMEM
    thin = part // 2
    scratch = [
        vmem((2, SPAN, block, width), BF16), vmem((SPAN, block, width), BF16), vmem((rows, width), BF16),
        vmem(sketch.shape, F32),
        vmem((width, width), F32), vmem((n_space, part, width), F32), vmem((n_k, 2, part, width), F32),
        vmem((n_space, part, width), BF16), vmem((n_space, part, width), BF16),
        vmem((SPAN, part, width), BF16), vmem((n_k, part, width), BF16),
        vmem((n_space, thin, width), BF16), vmem((n_space, thin, width), BF16),
        vmem((SPAN, thin, width), BF16), vmem((n_space, thin, width), BF16),
        vmem((n_space, thin, width), BF16), vmem((n_space, thin, width), BF16),
        vmem((n_group, thin, width), BF16), vmem((n_space, thin, width), BF16),
        vmem((2 * width, 2 * width), F32), vmem((2 * width, 2 * width), F32), vmem((2 * width, 2 * width), F32),
        vmem((2, 2, 2 * width, width), BF16), vmem((2, 2 * width, width), BF16),
        vmem((2, 2, block, width), BF16), vmem((2, block, width), BF16), vmem((2, block, width), BF16),
        vmem((2, width, width), F32), vmem((2, width, width), F32),
        dma((3, PIECES)), dma((3, PIECES)), dma((3,)), dma((3,)), dma((SPAN,)), dma((SPAN,)), dma((4,)),
        dma((n_k,)), dma((n_space,)), dma((SPAN,)), dma((2,)), dma((n_k,)), dma((n_k,)),
        dma((3, n_space)), dma((3, n_space)), dma((3, n_group)), dma((3, n_group)),
        dma((3, n_space)), dma((3, n_space)), dma((2,)), dma((2,)), dma((3, 2)), dma((3, 2)),
    ]
    return pl.pallas_call(
        functools.partial(kernel, n_space, n_group),
        out_shape=jax.ShapeDtypeStruct((block, width), BF16),
        in_specs=[pl.BlockSpec(memory_space=pl.ANY)] * 2,
        out_specs=pl.BlockSpec(memory_space=pltpu.VMEM),
        scratch_shapes=scratch,
        compiler_params=pltpu.CompilerParams(
            collective_id=0, has_side_effects=True, vmem_limit_bytes=56 * 1024 * 1024),
        name="merge",
    )(snapshot_basis, sketch)


def solution(mesh):
    in_specs = (P("space", "group"), P())
    out_specs = P(("space", "group"), None)
    step = functools.partial(body, mesh.shape["space"], mesh.shape["group"])
    return jax.shard_map(step, mesh=mesh, in_specs=in_specs, out_specs=out_specs, check_vma=False)
```

time: 151 us -> 131 us (0.87)
  Pallas kernels: 149 us -> 129 us
    pallas_call x1, Pallas kernels: 149 us -> 129 us  [body(): pl.pallas_call(functools.partial(kernel, n_space, n_group), out_shape=jax...]
where the time goes in v2:
time: 131 us
  Pallas kernels  129 us (98%)
  local copies, waits for them, and re-layouts  1.87 us (1%)
    pallas_call x1, Pallas kernels, body(): pl.pallas_call(functools.partial(kernel, n_space, n_group), out_shape=jax...  129 us

profile of v2, /device:TPU:1, one launch (start us, length us, event | category | flops | bytes accessed | tf_op | source)
XLA Modules:
  0.0 130.5 jit_solution(3717512485188092555)
XLA Ops:
  0.0 128.7 %merge.1 = bf16[1024,256]{1,0:T(8,128)(2,1)} custom-call(bf16[8192,256]{1,0:T(8,128)(2,1)} %x_hbm.1, f32[3,512,256]{2,1,0:T(8,128)} %sk_hbm.1), custom_call_target="tpu_custom_call" | custom-call | tf_op jit(solution)/shard_map/merge/pallas_call | solution.py:449
  128.7 1.9 %copy.4 = bf16[1024,256]{1,0:T(8,128)(2,1)} copy(bf16[1024,256]{1,0:T(8,128)(2,1)} %merge.1) | data formatting | bytes 1048576

commit v3 on v2

--- a/solution.py
+++ b/solution.py
@@ -14,6 +14,7 @@
 SPAN = 4
 PIECES = 4
 SPLIT = 2
+TILE = 512
 
 
 def dot(a, b):
@@ -55,7 +56,11 @@
 
 
 def mix_of(iterate, sketch):
-    return (0.5 * (sketch + dot(iterate.astype(BF16), sketch.astype(BF16)))).astype(BF16)
+    low = iterate.astype(BF16)
+    once = dot(low, sketch.astype(BF16))
+    twice = dot(low, once.astype(BF16))
+    thrice = dot(low, twice.astype(BF16))
+    return (0.5 * (sketch + 1.5 * once - 0.5 * thrice)).astype(BF16)
 
 
 def projected(gram, mix):
@@ -70,10 +75,10 @@
     x_hbm, sk_hbm, out_ref,
     panels, other, own, sketch, diag, diag_in, diag_all,
     cs0, cr0, cg0, ca0, cs1, cr1, cg1, ca1, cs2, cr2, cg2, ca2,
-    gram, gram1, it, mix0, mix1, p1, po, q, block1, block2,
+    gram, gram1, it, mix0, mix1, pf, q, block1, cross1, block2,
     a_send, a_recv, b_send, b_recv, f_send, f_recv, l_sem,
     dr_send, dr_recv, dg_send, dg_recv, da_send, da_recv,
-    r_send, r_recv, g_send, g_recv, k_send, k_recv, c_send, c_recv, z_send, z_recv,
+    r_send, r_recv, g_send, g_recv, k_send, k_recv, c_send, c_recv, z_send, z_recv, e_send, e_recv,
 ):
     s = lax.axis_index("space")
     g = lax.axis_index("group")
@@ -86,7 +91,6 @@
     gz = lax.div(g, SPAN)
     far = 1 - gz
     part = width // n_k
-    half = width
     partner = (2 * k + 1 - c, g)
 
     def remote(src, dst, send, recv, to):
@@ -263,51 +267,56 @@
     loop(1, n_k, lambda d: diag_gather(d).start())
     closing.append(lambda: loop(1, n_k, lambda d: diag_gather(d).wait_send()))
 
-    def reduce_cross(level, cs, cr, cg, ca, all_groups, everyone, beside):
-        mid, mids, mid_peer = (g, n_group, group_peer) if all_groups else (gx, SPAN, x_peer)
-        at, peers, peer = (s, n_space, space_peer) if everyone else (k, n_k, core_peer)
-
-        def scatter(d):
-            to = lax.rem(s + d, n_space)
-            return remote(cs.at[to], cr.at[s], r_send.at[level, d], r_recv.at[level, d], (to, g))
-
-        def share(d):
-            return remote(cg.at[mid], cg.at[mid], g_send.at[level, d], g_recv.at[level, d], mid_peer(d))
-
-        def gather(d):
-            return remote(ca.at[at], ca.at[at], k_send.at[level, d], k_recv.at[level, d], peer(d))
-
-        loop(1, n_space, lambda d: scatter(d).start())
-        cr[s] = cs[s]
-        beside[0]()
-        loop(1, n_space, lambda d: scatter(d).wait_recv())
-        cg[mid] = jnp.sum(cr[...].astype(F32), axis=0).astype(BF16)
-        loop(1, mids, lambda d: share(d).start())
-        beside[1]()
-        loop(1, mids, lambda d: share(d).wait_recv())
-        ca[at] = jnp.sum(cg[...].astype(F32), axis=0).astype(BF16)
-        loop(1, peers, lambda d: gather(d).start())
-        beside[2]()
-        loop(1, peers, lambda d: gather(d).wait_recv())
-
-        @closing.append
-        def _():
-            loop(1, n_space, lambda d: scatter(d).wait_send())
-            loop(1, mids, lambda d: share(d).wait_send())
-            loop(1, peers, lambda d: gather(d).wait_send())
-
-    tile = 256
+    class CrossSum:
+        def __init__(self, level, cs, cr, cg, ca, all_groups, everyone):
+            mid, self.mids, mid_peer = (g, n_group, group_peer) if all_groups else (gx, SPAN, x_peer)
+            at, self.peers, peer = (s, n_space, space_peer) if everyone else (k, n_k, core_peer)
+            self.cs, self.cr, self.cg, self.ca, self.mid, self.at = cs, cr, cg, ca, mid, at
+
+            def scatter(d):
+                to = lax.rem(s + d, n_space)
+                return remote(cs.at[to], cr.at[s], r_send.at[level, d], r_recv.at[level, d], (to, g))
+
+            def share(d):
+                return remote(cg.at[mid], cg.at[mid], g_send.at[level, d], g_recv.at[level, d], mid_peer(d))
+
+            def gather(d):
+                return remote(ca.at[at], ca.at[at], k_send.at[level, d], k_recv.at[level, d], peer(d))
+
+            self.scatter, self.share, self.gather = scatter, share, gather
+
+        def begin(self):
+            loop(1, n_space, lambda d: self.scatter(d).start())
+            self.cr[s] = self.cs[s]
+
+            @closing.append
+            def _():
+                loop(1, n_space, lambda d: self.scatter(d).wait_send())
+                loop(1, self.mids, lambda d: self.share(d).wait_send())
+                loop(1, self.peers, lambda d: self.gather(d).wait_send())
+
+        def to_share(self):
+            loop(1, n_space, lambda d: self.scatter(d).wait_recv())
+            self.cg[self.mid] = jnp.sum(self.cr[...].astype(F32), axis=0).astype(BF16)
+            loop(1, self.mids, lambda d: self.share(d).start())
+
+        def to_gather(self):
+            loop(1, self.mids, lambda d: self.share(d).wait_recv())
+            self.ca[self.at] = jnp.sum(self.cg[...].astype(F32), axis=0).astype(BF16)
+            loop(1, self.peers, lambda d: self.gather(d).start())
+
+        def end(self):
+            loop(1, self.peers, lambda d: self.gather(d).wait_recv())
 
     def mixed(a, b, mix, dst):
-        upper, lower = mix[:width, :], mix[width:, :]
-
-        def rows(j):
-            here = pl.ds(pl.multiple_of(j * tile, tile), tile)
-            dst[here, :] = (dot(a[here, :], upper) + dot(b[here, :], lower)).astype(BF16)
-
-        loop(0, block // tile, rows)
-
-    def filtered(upper, cross, lower, test, into):
+        for j in range(block // TILE):
+            rows = pl.ds(j * TILE, TILE)
+            dst[rows, :] = (dot(a[rows, :], mix[:width, :]) + dot(b[rows, :], mix[width:, :])).astype(BF16)
+
+    def nothing():
+        pass
+
+    def filtered(upper, cross, lower, test, into, midway=nothing):
         into[:width, :width] = upper
         into[width:, width:] = lower
         into[:width, width:] = cross
@@ -317,105 +326,118 @@
         def step(_):
             it[...] = filter_step(it[...])
 
-        loop(0, STEPS, step)
+        loop(0, 2, step)
+        midway()
+        loop(2, STEPS - 1, step)
         return mix_of(it[...], test)
-
-    def nothing():
-        pass
 
     for d in (1, 2, 3):
         second(d).wait_recv()
     first_last = PIECES - 1
     for d in (1, 2, 3):
         first(d, first_last).wait_recv()
+    sum0 = CrossSum(0, cs0, cr0, cg0, ca0, False, False)
+    sum1 = CrossSum(1, cs1, cr1, cg1, ca1, False, False)
+    sum2 = CrossSum(2, cs2, cr2, cg2, ca2, True, True)
+
+    def raw_cross(a, b):
+        cross = dot_t(panels[0, a], panels[0, b]) + dot_t(panels[1, a], panels[1, b])
+        return cross.astype(BF16).reshape(n_k, part, width)
+
     for i in range(2):
-        cross = dot_t(panels[0, 2 * i], panels[0, 2 * i + 1]) + dot_t(panels[1, 2 * i], panels[1, 2 * i + 1])
-        cross = cross.astype(BF16).reshape(n_k, part, width)
+        cross = raw_cross(2 * i, 2 * i + 1)
         for kk in range(n_k):
             cs0[2 * kk + i] = cross[kk]
-
-    def pass_last():
-        for d in (2, 1, 3):
-            pass_rows(d, first_last * piece, piece).start()
-
-    reduce_cross(0, cs0, cr0, cg0, ca0, False, False, (
-        pass_last, lambda: loop(1, n_k, lambda d: diag_gather(d).wait_recv()), nothing))
+    sum0.begin()
+    for i in range(2):
+        for j in range(2):
+            cross = raw_cross(i, 2 + j)
+            for kk in range(n_k):
+                cs1[2 * kk + i, j] = cross[kk]
+    sum0.to_share()
+    sum1.begin()
+    for d in (2, 1, 3):
+        pass_rows(d, first_last * piece, piece).start()
+    loop(1, n_k, lambda d: diag_gather(d).wait_recv())
+    sum0.to_gather()
+    sum1.to_share()
     tests.wait()
+    sum0.end()
     mix0[0, c] = filtered(
         diag_all[:, 0].reshape(width, width), ca0[...].astype(F32).reshape(width, width),
-        diag_all[:, 1].reshape(width, width), sketch[0], gram)
+        diag_all[:, 1].reshape(width, width), sketch[0], gram, sum1.to_gather)
     swap0 = remote(mix0.at[0, c], mix0.at[0, c], c_send.at[0], c_recv.at[0], partner)
     swap0.start()
-    closing.append(swap0.wait_send)
-
-    def cross_z(n, src, dst):
-        def copy(core):
-            return remote(src, dst, z_send.at[n, core], z_recv.at[n, c], z_peer(core))
-
-        def arrived(core, into):
-            return remote(into, into, z_send.at[n, 0], z_recv.at[n, core], z_peer(core))
-
-        loop(0, 2, lambda core: copy(core).start())
-        closing.append(lambda: loop(0, 2, lambda core: copy(core).wait_send()))
-        return arrived
-
-    mixes = cross_z(0, mix0.at[0, c], mix0.at[1, c])
-
-    def first_merge(pair):
-        for h in range(2):
-            mixed(panels.at[h, 2 * pair], panels.at[h, 2 * pair + 1], mix0.at[0, pair], p1.at[h, pair])
-
-    first_merge(c)
+    mixes = remote(mix0.at[0, c], mix0.at[1, c], z_send.at[0], z_recv.at[0], z_peer(c))
+    mixes.start()
+
+    block1[c] = projected(gram[...], mix0[0, c])
+    swap1 = remote(block1.at[c], block1.at[c], c_send.at[1], c_recv.at[1], partner)
+    swap1.start()
+    mixed(panels.at[gz, 2 * c], panels.at[gz, 2 * c + 1], mix0.at[0, c], pf.at[gz, c])
     swap0.wait_recv()
-    first_merge(1 - c)
-    cross = dot_t(p1[0, 0], p1[0, 1]) + dot_t(p1[1, 0], p1[1, 1])
-    cs1[...] = cross.astype(BF16).reshape(n_space, part // 2, width)
-    swap1 = remote(block1.at[c], block1.at[c], c_send.at[1], c_recv.at[1], partner)
-
-    def diag1():
-        block1[c] = projected(gram[...], mix0[0, c])
-        swap1.start()
-
-    def other_rows():
-        for core in range(2):
-            mixes(core, mix0.at[1, core]).wait_recv()
-        for d in range(SPAN):
-            pass_rows(d, 0, block).wait_recv()
-        for pair in range(2):
-            mixed(other.at[2 * pair], other.at[2 * pair + 1], mix0.at[1, pair], po.at[pair])
-
-    reduce_cross(1, cs1, cr1, cg1, ca1, False, True, (diag1, nothing, other_rows))
+    mixed(panels.at[gz, 2 - 2 * c], panels.at[gz, 3 - 2 * c], mix0.at[0, 1 - c], pf.at[gz, 1 - c])
+    sum1.end()
+    raw = ca1[...]
+    high, low = split(
+        dot(raw[:, 0].reshape(width, width), mix0[0, 1, :width, :])
+        + dot(raw[:, 1].reshape(width, width), mix0[0, 1, width:, :]))
+    left = mix0[0, 0, pl.ds(pl.multiple_of(c * width, width), width), :]
+    cross1[c] = dot_t(left, high) + dot_t(left, low)
+    swap2 = remote(cross1.at[c], cross1.at[c], c_send.at[2], c_recv.at[2], partner)
+    swap2.start()
     swap1.wait_recv()
-    closing.append(swap1.wait_send)
-    mix1[0] = filtered(
-        block1[0], ca1[...].astype(F32).reshape(width, width), block1[1], sketch[1], gram1)
-    mine_half = pl.ds(pl.multiple_of(c * half, half), half)
-    merges = cross_z(1, mix1.at[0, mine_half], mix1.at[1, mine_half])
-
-    mixed(p1.at[gz, 0], p1.at[gz, 1], mix1.at[0], q.at[gz])
-    for core in range(2):
-        merges(core, mix1.at[1, pl.ds(core * half, half)]).wait_recv()
-    mixed(po.at[0], po.at[1], mix1.at[1], q.at[far])
+    swap2.wait_recv()
+    mix1[0] = filtered(block1[0], cross1[0] + cross1[1], block1[1], sketch[1], gram1)
+    my_half = pl.ds(pl.multiple_of(c * width, width), width)
+    merges = remote(mix1.at[0, my_half], mix1.at[1, my_half], z_send.at[1], z_recv.at[1], z_peer(c))
+    merges.start()
+    mixes.wait_recv()
+    swap3 = remote(mix0.at[1, c], mix0.at[1, c], c_send.at[3], c_recv.at[3], partner)
+    swap3.start()
+
+    mixed(pf.at[gz, 0], pf.at[gz, 1], mix1.at[0], q.at[gz])
+    for d in range(SPAN):
+        pass_rows(d, 0, block).wait_recv()
+    mixed(other.at[2 * c], other.at[2 * c + 1], mix0.at[1, c], pf.at[far, c])
+    swap3.wait_recv()
+    mixed(other.at[2 - 2 * c], other.at[3 - 2 * c], mix0.at[1, 1 - c], pf.at[far, 1 - c])
+    merges.wait_recv()
+    swap4 = remote(mix1.at[1, my_half], mix1.at[1, my_half], c_send.at[4], c_recv.at[4], partner)
+    swap4.start()
+    swap4.wait_recv()
+    mixed(pf.at[far, 0], pf.at[far, 1], mix1.at[1], q.at[far])
+
+    @closing.append
+    def _():
+        for copy in (swap0, swap1, swap2, swap3, swap4, mixes, merges):
+            copy.wait_send()
+
     cs2[...] = dot_t(q[0], q[1]).astype(BF16).reshape(n_space, part // 2, width)
-    rows2 = pl.ds(pl.multiple_of(c * (width // 2), width // 2), width // 2)
-    later = []
-
-    def diag2():
-        block2[gz] = projected(gram1[...], mix1[0])
-        later.append(cross_z(2, block2.at[gz, rows2], block2.at[gz, rows2]))
-
-    reduce_cross(2, cs2, cr2, cg2, ca2, True, True, (diag2, nothing, nothing))
-    for core in range(2):
-        later[0](core, block2.at[far, pl.ds(core * (width // 2), width // 2)]).wait_recv()
+    sum2.begin()
+    block2[gz] = projected(gram1[...], mix1[0])
+    strip = width // 2
+
+    def strip_copy(core):
+        rows = pl.ds(pl.multiple_of(c * strip, strip), strip)
+        return remote(block2.at[gz, rows], block2.at[gz, rows], e_send.at[core], e_recv.at[c], z_peer(core))
+
+    def strip_arrived(core):
+        rows = pl.ds(pl.multiple_of(core * strip, strip), strip)
+        return remote(block2.at[far, rows], block2.at[far, rows], e_send.at[0], e_recv.at[core], z_peer(core))
+
+    loop(0, 2, lambda core: strip_copy(core).start())
+    closing.append(lambda: loop(0, 2, lambda core: strip_copy(core).wait_send()))
+    sum2.to_share()
+    sum2.to_gather()
+    loop(0, 2, lambda core: strip_arrived(core).wait_recv())
+    sum2.end()
     last = filtered(
         block2[0], ca2[...].astype(F32).reshape(width, width), block2[1], sketch[2], gram)
     upper, lower = last[:width, :], last[width:, :]
-
-    def rows(j):
-        here = pl.ds(pl.multiple_of(j * tile, tile), tile)
-        out_ref[here, :] = (dot(q[0, here, :], upper) + dot(q[1, here, :], lower)).astype(BF16)
-
-    loop(0, block // tile, rows)
+    for j in range(block // TILE):
+        rows = pl.ds(j * TILE, TILE)
+        out_ref[rows, :] = (dot(q[0, rows, :], upper) + dot(q[1, rows, :], lower)).astype(BF16)
     finish()
 
 
@@ -433,18 +455,18 @@
         vmem((width, width), F32), vmem((n_space, part, width), F32), vmem((n_k, 2, part, width), F32),
         vmem((n_space, part, width), BF16), vmem((n_space, part, width), BF16),
         vmem((SPAN, part, width), BF16), vmem((n_k, part, width), BF16),
-        vmem((n_space, thin, width), BF16), vmem((n_space, thin, width), BF16),
-        vmem((SPAN, thin, width), BF16), vmem((n_space, thin, width), BF16),
+        vmem((n_space, 2, part, width), BF16), vmem((n_space, 2, part, width), BF16),
+        vmem((SPAN, 2, part, width), BF16), vmem((n_k, 2, part, width), BF16),
         vmem((n_space, thin, width), BF16), vmem((n_space, thin, width), BF16),
         vmem((n_group, thin, width), BF16), vmem((n_space, thin, width), BF16),
         vmem((2 * width, 2 * width), F32), vmem((2 * width, 2 * width), F32), vmem((2 * width, 2 * width), F32),
         vmem((2, 2, 2 * width, width), BF16), vmem((2, 2 * width, width), BF16),
-        vmem((2, 2, block, width), BF16), vmem((2, block, width), BF16), vmem((2, block, width), BF16),
-        vmem((2, width, width), F32), vmem((2, width, width), F32),
+        vmem((2, 2, block, width), BF16), vmem((2, block, width), BF16),
+        vmem((2, width, width), F32), vmem((2, width, width), F32), vmem((2, width, width), F32),
         dma((3, PIECES)), dma((3, PIECES)), dma((3,)), dma((3,)), dma((SPAN,)), dma((SPAN,)), dma((4,)),
         dma((n_k,)), dma((n_space,)), dma((SPAN,)), dma((2,)), dma((n_k,)), dma((n_k,)),
         dma((3, n_space)), dma((3, n_space)), dma((3, n_group)), dma((3, n_group)),
-        dma((3, n_space)), dma((3, n_space)), dma((2,)), dma((2,)), dma((3, 2)), dma((3, 2)),
+        dma((3, n_space)), dma((3, n_space)), dma((5,)), dma((5,)), dma((2,)), dma((2,)), dma((2,)), dma((2,)),
     ]
     return pl.pallas_call(
         functools.partial(kernel, n_space, n_group),

time: 131 us -> 125 us (0.954)
  Pallas kernels: 129 us -> 123 us
    pallas_call x1, Pallas kernels: 129 us -> 123 us  [body(): pl.pallas_call(functools.partial(kernel, n_space, n_group), out_shape=jax...]
where the time goes in v3:
time: 125 us
  Pallas kernels  123 us (98%)
  local copies, waits for them, and re-layouts  1.87 us (1%)
    pallas_call x1, Pallas kernels, body(): pl.pallas_call(functools.partial(kernel, n_space, n_group), out_shape=jax...  123 us

profile of v3, /device:TPU:1, one launch (start us, length us, event | category | flops | bytes accessed | tf_op | source)
XLA Modules:
  0.0 125.1 jit_solution(11326637911060531416)
XLA Ops:
  0.0 123.2 %merge.1 = bf16[1024,256]{1,0:T(8,128)(2,1)} custom-call(bf16[8192,256]{1,0:T(8,128)(2,1)} %x_hbm.1, f32[3,512,256]{2,1,0:T(8,128)} %sk_hbm.1), custom_call_target="tpu_custom_call" | custom-call | tf_op jit(solution)/shard_map/merge/pallas_call | solution.py:471
  123.2 1.9 %copy.4 = bf16[1024,256]{1,0:T(8,128)(2,1)} copy(bf16[1024,256]{1,0:T(8,128)(2,1)} %merge.1) | data formatting | bytes 1048576

commit v4 on v3

--- a/solution.py
+++ b/solution.py
@@ -12,8 +12,8 @@
 F32 = jnp.float32
 BF16 = jnp.bfloat16
 SPAN = 4
-PIECES = 4
-SPLIT = 2
+PIECES = 8
+SPLIT = 1
 TILE = 512
 
 
@@ -38,15 +38,33 @@
     lax.fori_loop(low, high, step, 0)
 
 
-def start_of_filter(gram):
-    width = gram.shape[0]
-    row = lax.broadcasted_iota(jnp.int32, gram.shape, 0)
-    col = lax.broadcasted_iota(jnp.int32, gram.shape, 1)
+def total(a):
+    return jnp.sum(a, axis=(0, 1), keepdims=True)
+
+
+def diagonal_of_filter(upper, lower, into):
+    width = upper.shape[0]
+    row = lax.broadcasted_iota(jnp.int32, upper.shape, 0)
+    col = lax.broadcasted_iota(jnp.int32, upper.shape, 1)
     eye = row == col
-    trace = jnp.sum(jnp.where(eye, gram, 0.0), axis=(0, 1), keepdims=True)
-    shifted = gram * (1.0 / (trace / width)) - jnp.where(eye, 1.0, 0.0)
-    norm = jnp.sqrt(jnp.sum(shifted * shifted, axis=(0, 1), keepdims=True))
-    return shifted * (1.0 / (1.0 + norm))
+    scale = 1.0 / (total(jnp.where(eye, upper + lower, 0.0)) / (2 * width))
+    one = jnp.where(eye, 1.0, 0.0)
+    upper = upper * scale - one
+    lower = lower * scale - one
+    into[:width, :width] = upper
+    into[width:, width:] = lower
+    return scale, total(upper * upper + lower * lower)
+
+
+def start_of_filter(scale, squares, cross, into):
+    width = cross.shape[0]
+    cross = cross * scale
+    factor = 1.0 / (1.0 + jnp.sqrt(squares + 2.0 * total(cross * cross)))
+    cross = cross * factor
+    into[:width, width:] = cross
+    into[width:, :width] = cross.T
+    into[:width, :width] = into[:width, :width] * factor
+    into[width:, width:] = into[width:, width:] * factor
 
 
 def filter_step(iterate):
@@ -149,7 +167,7 @@
     def x_copy(d, h, at, size, send, recv):
         to = lax.rem(gx + d, SPAN)
         return remote(
-            x_hbm.at[pl.ds(pl.multiple_of((h * SPAN + to) * block + at, size), size)],
+            own.at[pl.ds(pl.multiple_of((h * SPAN + to) * block + at, size), size)],
             panels.at[h, gx, pl.ds(pl.multiple_of(at, size), size)],
             send, recv, (s, gz * SPAN + to))
 
@@ -170,6 +188,7 @@
             x_copy(d, gz, j * (piece // SPLIT), piece // SPLIT,
                    b_send.at[d - 1], b_recv.at[d - 1]).start()
 
+    whole.wait()
     loop(0, PIECES * SPLIT, send_first)
 
     @closing.append
@@ -189,12 +208,18 @@
             first(d, p).wait_recv()
             pass_rows(d, p * piece, piece).start()
 
+    def pass_own(at, size):
+        rows = pl.ds(pl.multiple_of((far * SPAN + gx) * block + at, size), size)
+        remote(own.at[rows], other.at[gx, pl.ds(at, size)], f_send.at[0], f_recv.at[0],
+               (s, far * SPAN + gx)).start()
+
+    pass_own(0, block // 2)
+
     @closing.append
     def _():
         for d in range(SPAN):
             pass_rows(d, 0, block).wait_send()
 
-    whole.wait()
     diag[...] = jnp.zeros_like(diag)
 
     def add_diag(j):
@@ -221,7 +246,7 @@
 
     mine(0).wait()
     mine(1).wait()
-    pass_rows(0, 0, block).start()
+    pass_own(block // 2, block // 2)
 
     def pass_diag(d):
         return remote(diag_all.at[k, slot], diag_all.at[k, slot], dg_send.at[d], dg_recv.at[slot],
@@ -251,7 +276,7 @@
             loop(1, SPAN, lambda d: pass_diag(d).wait_send())
 
     loop(0, PIECES * SPLIT, send_second)
-    loop(0, PIECES - 1, pass_piece)
+    loop(0, PIECES - 2, pass_piece)
 
     def diag_arrived(j):
         @pl.when(2 * c + j != gx)
@@ -266,6 +291,7 @@
 
     loop(1, n_k, lambda d: diag_gather(d).start())
     closing.append(lambda: loop(1, n_k, lambda d: diag_gather(d).wait_send()))
+    pass_piece(PIECES - 2)
 
     class CrossSum:
         def __init__(self, level, cs, cr, cg, ca, all_groups, everyone):
@@ -316,20 +342,22 @@
     def nothing():
         pass
 
-    def filtered(upper, cross, lower, test, into, midway=nothing):
+    def filtered(scale, squares, cross, test, midway=nothing):
+        start_of_filter(scale, squares, cross, it)
+
+        def step(_):
+            it[...] = filter_step(it[...])
+
+        loop(0, 2, step)
+        midway()
+        loop(2, STEPS - 1, step)
+        return mix_of(it[...], test)
+
+    def keep(into, upper, cross, lower):
         into[:width, :width] = upper
         into[width:, width:] = lower
         into[:width, width:] = cross
         into[width:, :width] = cross.T
-        it[...] = start_of_filter(into[...])
-
-        def step(_):
-            it[...] = filter_step(it[...])
-
-        loop(0, 2, step)
-        midway()
-        loop(2, STEPS - 1, step)
-        return mix_of(it[...], test)
 
     for d in (1, 2, 3):
         second(d).wait_recv()
@@ -354,29 +382,35 @@
             cross = raw_cross(i, 2 + j)
             for kk in range(n_k):
                 cs1[2 * kk + i, j] = cross[kk]
+    sum1.begin()
     sum0.to_share()
-    sum1.begin()
+    loop(1, n_k, lambda d: diag_gather(d).wait_recv())
+    sum0.to_gather()
     for d in (2, 1, 3):
         pass_rows(d, first_last * piece, piece).start()
-    loop(1, n_k, lambda d: diag_gather(d).wait_recv())
-    sum0.to_gather()
     sum1.to_share()
     tests.wait()
+    upper, lower = (diag_all[:, j].reshape(width, width) for j in range(2))
+    scale, squares = diagonal_of_filter(upper, lower, it)
     sum0.end()
-    mix0[0, c] = filtered(
-        diag_all[:, 0].reshape(width, width), ca0[...].astype(F32).reshape(width, width),
-        diag_all[:, 1].reshape(width, width), sketch[0], gram, sum1.to_gather)
+
+    cross = ca0[...].astype(F32).reshape(width, width)
+    mix0[0, c] = filtered(scale, squares, cross, sketch[0], sum1.to_gather)
     swap0 = remote(mix0.at[0, c], mix0.at[0, c], c_send.at[0], c_recv.at[0], partner)
     swap0.start()
     mixes = remote(mix0.at[0, c], mix0.at[1, c], z_send.at[0], z_recv.at[0], z_peer(c))
     mixes.start()
 
+    keep(gram, *(diag_all[:, 0].reshape(width, width), ca0[...].astype(F32).reshape(width, width),
+                 diag_all[:, 1].reshape(width, width)))
     block1[c] = projected(gram[...], mix0[0, c])
     swap1 = remote(block1.at[c], block1.at[c], c_send.at[1], c_recv.at[1], partner)
     swap1.start()
     mixed(panels.at[gz, 2 * c], panels.at[gz, 2 * c + 1], mix0.at[0, c], pf.at[gz, c])
     swap0.wait_recv()
     mixed(panels.at[gz, 2 - 2 * c], panels.at[gz, 3 - 2 * c], mix0.at[0, 1 - c], pf.at[gz, 1 - c])
+    swap1.wait_recv()
+    scale, squares = diagonal_of_filter(block1[0], block1[1], it)
     sum1.end()
     raw = ca1[...]
     high, low = split(
@@ -386,12 +420,16 @@
     cross1[c] = dot_t(left, high) + dot_t(left, low)
     swap2 = remote(cross1.at[c], cross1.at[c], c_send.at[2], c_recv.at[2], partner)
     swap2.start()
-    swap1.wait_recv()
     swap2.wait_recv()
-    mix1[0] = filtered(block1[0], cross1[0] + cross1[1], block1[1], sketch[1], gram1)
+    mix1[0] = filtered(scale, squares, cross1[0] + cross1[1], sketch[1])
     my_half = pl.ds(pl.multiple_of(c * width, width), width)
     merges = remote(mix1.at[0, my_half], mix1.at[1, my_half], z_send.at[1], z_recv.at[1], z_peer(c))
     merges.start()
+    keep(gram1, block1[0], cross1[0] + cross1[1], block1[1])
+    block2[gz] = projected(gram1[...], mix1[0])
+    strip = pl.ds(pl.multiple_of(c * (width // 2), width // 2), width // 2)
+    strips = remote(block2.at[gz, strip], block2.at[gz, strip], e_send.at[0], e_recv.at[0], z_peer(c))
+    strips.start()
     mixes.wait_recv()
     swap3 = remote(mix0.at[1, c], mix0.at[1, c], c_send.at[3], c_recv.at[3], partner)
     swap3.start()
@@ -410,30 +448,21 @@
 
     @closing.append
     def _():
-        for copy in (swap0, swap1, swap2, swap3, swap4, mixes, merges):
+        for copy in (swap0, swap1, swap2, swap3, swap4, mixes, merges, strips):
             copy.wait_send()
 
     cs2[...] = dot_t(q[0], q[1]).astype(BF16).reshape(n_space, part // 2, width)
     sum2.begin()
-    block2[gz] = projected(gram1[...], mix1[0])
-    strip = width // 2
-
-    def strip_copy(core):
-        rows = pl.ds(pl.multiple_of(c * strip, strip), strip)
-        return remote(block2.at[gz, rows], block2.at[gz, rows], e_send.at[core], e_recv.at[c], z_peer(core))
-
-    def strip_arrived(core):
-        rows = pl.ds(pl.multiple_of(core * strip, strip), strip)
-        return remote(block2.at[far, rows], block2.at[far, rows], e_send.at[0], e_recv.at[core], z_peer(core))
-
-    loop(0, 2, lambda core: strip_copy(core).start())
-    closing.append(lambda: loop(0, 2, lambda core: strip_copy(core).wait_send()))
+    remote(block2.at[far, strip], block2.at[far, strip], e_send.at[0], e_recv.at[0], z_peer(c)).wait_recv()
+    swap5 = remote(block2.at[far, strip], block2.at[far, strip], e_send.at[1], e_recv.at[1], partner)
+    swap5.start()
+    closing.append(swap5.wait_send)
     sum2.to_share()
     sum2.to_gather()
-    loop(0, 2, lambda core: strip_arrived(core).wait_recv())
+    swap5.wait_recv()
+    scale, squares = diagonal_of_filter(block2[0], block2[1], it)
     sum2.end()
-    last = filtered(
-        block2[0], ca2[...].astype(F32).reshape(width, width), block2[1], sketch[2], gram)
+    last = filtered(scale, squares, ca2[...].astype(F32).reshape(width, width), sketch[2])
     upper, lower = last[:width, :], last[width:, :]
     for j in range(block // TILE):
         rows = pl.ds(j * TILE, TILE)

time: 125 us -> 120 us (0.960)
  Pallas kernels: 123 us -> 118 us
    pallas_call x1, Pallas kernels: 123 us -> 118 us  [body(): pl.pallas_call(functools.partial(kernel, n_space, n_group), out_shape=jax...]
where the time goes in v4:
time: 120 us
  Pallas kernels  118 us (98%)
  local copies, waits for them, and re-layouts  1.87 us (2%)
    pallas_call x1, Pallas kernels, body(): pl.pallas_call(functools.partial(kernel, n_space, n_group), out_shape=jax...  118 us

profile of v4, /device:TPU:1, one launch (start us, length us, event | category | flops | bytes accessed | tf_op | source)
XLA Modules:
  0.0 119.8 jit_solution(10935729146347032832)
XLA Ops:
  0.0 117.9 %merge.1 = bf16[1024,256]{1,0:T(8,128)(2,1)} custom-call(bf16[8192,256]{1,0:T(8,128)(2,1)} %x_hbm.1, f32[3,512,256]{2,1,0:T(8,128)} %sk_hbm.1), custom_call_target="tpu_custom_call" | custom-call | tf_op jit(solution)/shard_map/merge/pallas_call | solution.py:500
  117.9 1.9 %copy.4 = bf16[1024,256]{1,0:T(8,128)(2,1)} copy(bf16[1024,256]{1,0:T(8,128)(2,1)} %merge.1) | data formatting | bytes 1048576

commit v5 on v4

--- a/solution.py
+++ b/solution.py
@@ -67,10 +67,18 @@
     into[width:, width:] = into[width:, width:] * factor
 
 
-def filter_step(iterate):
-    low = iterate.astype(BF16)
-    square = dot(low, low).astype(BF16)
-    return 1.5 * iterate - 0.5 * dot(square, low)
+def filter_step(iterate, low, square):
+    width = iterate.shape[0] // 2
+    a, b = pl.ds(0, width), pl.ds(width, width)
+    low[...] = iterate[...].astype(BF16)
+    square[a, :] = dot(low[a, :], low[...]).astype(BF16)
+    square[b, b] = dot(low[b, :], low[:, b]).astype(BF16)
+    square[b, a] = square[a, b].T
+    top = dot(square[a, :], low[...])
+    corner = dot(square[b, :], low[:, b])
+    iterate[a, :] = 1.5 * iterate[a, :] - 0.5 * top
+    iterate[b, b] = 1.5 * iterate[b, b] - 0.5 * corner
+    iterate[b, a] = iterate[a, b].T
 
 
 def mix_of(iterate, sketch):
@@ -93,7 +101,7 @@
     x_hbm, sk_hbm, out_ref,
     panels, other, own, sketch, diag, diag_in, diag_all,
     cs0, cr0, cg0, ca0, cs1, cr1, cg1, ca1, cs2, cr2, cg2, ca2,
-    gram, gram1, it, mix0, mix1, pf, q, block1, cross1, block2,
+    gram, gram1, it, low, square, mix0, mix1, pf, q, block1, cross1, block2,
     a_send, a_recv, b_send, b_recv, f_send, f_recv, l_sem,
     dr_send, dr_recv, dg_send, dg_recv, da_send, da_recv,
     r_send, r_recv, g_send, g_recv, k_send, k_recv, c_send, c_recv, z_send, z_recv, e_send, e_recv,
@@ -346,7 +354,7 @@
         start_of_filter(scale, squares, cross, it)
 
         def step(_):
-            it[...] = filter_step(it[...])
+            filter_step(it, low, square)
 
         loop(0, 2, step)
         midway()
@@ -413,11 +421,11 @@
     scale, squares = diagonal_of_filter(block1[0], block1[1], it)
     sum1.end()
     raw = ca1[...]
-    high, low = split(
+    high, rest = split(
         dot(raw[:, 0].reshape(width, width), mix0[0, 1, :width, :])
         + dot(raw[:, 1].reshape(width, width), mix0[0, 1, width:, :]))
     left = mix0[0, 0, pl.ds(pl.multiple_of(c * width, width), width), :]
-    cross1[c] = dot_t(left, high) + dot_t(left, low)
+    cross1[c] = dot_t(left, high) + dot_t(left, rest)
     swap2 = remote(cross1.at[c], cross1.at[c], c_send.at[2], c_recv.at[2], partner)
     swap2.start()
     swap2.wait_recv()
@@ -489,6 +497,7 @@
         vmem((n_space, thin, width), BF16), vmem((n_space, thin, width), BF16),
         vmem((n_group, thin, width), BF16), vmem((n_space, thin, width), BF16),
         vmem((2 * width, 2 * width), F32), vmem((2 * width, 2 * width), F32), vmem((2 * width, 2 * width), F32),
+        vmem((2 * width, 2 * width), BF16), vmem((2 * width, 2 * width), BF16),
         vmem((2, 2, 2 * width, width), BF16), vmem((2, 2 * width, width), BF16),
         vmem((2, 2, block, width), BF16), vmem((2, block, width), BF16),
         vmem((2, width, width), F32), vmem((2, width, width), F32), vmem((2, width, width), F32),
@@ -504,7 +513,7 @@
         out_specs=pl.BlockSpec(memory_space=pltpu.VMEM),
         scratch_shapes=scratch,
         compiler_params=pltpu.CompilerParams(
-            collective_id=0, has_side_effects=True, vmem_limit_bytes=56 * 1024 * 1024),
+            collective_id=0, has_side_effects=True, vmem_limit_bytes=53 * 1024 * 1024),
         name="merge",
     )(snapshot_basis, sketch)
 

time: 120 us -> 117 us (0.975)
    pallas_call x1, Pallas kernels: 118 us -> 117 us  [body(): pl.pallas_call(functools.partial(kernel, n_space, n_group), out_shape=jax...]
where the time goes in v5:
time: 117 us
  Pallas kernels  117 us (100%)
    pallas_call x1, Pallas kernels, body(): pl.pallas_call(functools.partial(kernel, n_space, n_group), out_shape=jax...  117 us

profile of v5, /device:TPU:1, one launch (start us, length us, event | category | flops | bytes accessed | tf_op | source)
XLA Modules:
  0.0 117.3 jit_solution(8285279499389558399)
XLA Ops:
  0.0 116.5 %merge.1 = bf16[1024,256]{1,0:T(8,128)(2,1)S(1)} custom-call(bf16[8192,256]{1,0:T(8,128)(2,1)} %x_hbm.1, f32[3,512,256]{2,1,0:T(8,128)} %sk_hbm.1), custom_call_target="tpu_custom_call" | custom-call | tf_op jit(solution)/shard_map/merge/pallas_call | solution.py:509
  116.5 0.8 copy.4

commit v6 on v5

--- a/solution.py
+++ b/solution.py
@@ -100,7 +100,7 @@
     n_space, n_group,
     x_hbm, sk_hbm, out_ref,
     panels, other, own, sketch, diag, diag_in, diag_all,
-    cs0, cr0, cg0, ca0, cs1, cr1, cg1, ca1, cs2, cr2, cg2, ca2,
+    cs0, cn0, cb0, cr0, cg0, ca0, cs1, cn1, cb1, cr1, cg1, ca1, cs2, cr2, cg2, ca2,
     gram, gram1, it, low, square, mix0, mix1, pf, q, block1, cross1, block2,
     a_send, a_recv, b_send, b_recv, f_send, f_recv, l_sem,
     dr_send, dr_recv, dg_send, dg_recv, da_send, da_recv,
@@ -302,14 +302,16 @@
     pass_piece(PIECES - 2)
 
     class CrossSum:
-        def __init__(self, level, cs, cr, cg, ca, all_groups, everyone):
+        def __init__(self, level, cs, cr, cg, ca, all_groups, everyone, both_cores=True):
             mid, self.mids, mid_peer = (g, n_group, group_peer) if all_groups else (gx, SPAN, x_peer)
             at, self.peers, peer = (s, n_space, space_peer) if everyone else (k, n_k, core_peer)
             self.cs, self.cr, self.cg, self.ca, self.mid, self.at = cs, cr, cg, ca, mid, at
+            self.own, self.senders = (s, n_space) if both_cores else (k, n_k)
 
             def scatter(d):
-                to = lax.rem(s + d, n_space)
-                return remote(cs.at[to], cr.at[s], r_send.at[level, d], r_recv.at[level, d], (to, g))
+                to = lax.rem(self.own + d, self.senders)
+                return remote(cs.at[to], cr.at[self.own], r_send.at[level, d], r_recv.at[level, d],
+                              space_peer(d) if both_cores else core_peer(d))
 
             def share(d):
                 return remote(cg.at[mid], cg.at[mid], g_send.at[level, d], g_recv.at[level, d], mid_peer(d))
@@ -320,17 +322,17 @@
             self.scatter, self.share, self.gather = scatter, share, gather
 
         def begin(self):
-            loop(1, n_space, lambda d: self.scatter(d).start())
-            self.cr[s] = self.cs[s]
+            loop(1, self.senders, lambda d: self.scatter(d).start())
+            self.cr[self.own] = self.cs[self.own]
 
             @closing.append
             def _():
-                loop(1, n_space, lambda d: self.scatter(d).wait_send())
+                loop(1, self.senders, lambda d: self.scatter(d).wait_send())
                 loop(1, self.mids, lambda d: self.share(d).wait_send())
                 loop(1, self.peers, lambda d: self.gather(d).wait_send())
 
         def to_share(self):
-            loop(1, n_space, lambda d: self.scatter(d).wait_recv())
+            loop(1, self.senders, lambda d: self.scatter(d).wait_recv())
             self.cg[self.mid] = jnp.sum(self.cr[...].astype(F32), axis=0).astype(BF16)
             loop(1, self.mids, lambda d: self.share(d).start())
 
@@ -372,24 +374,29 @@
     first_last = PIECES - 1
     for d in (1, 2, 3):
         first(d, first_last).wait_recv()
-    sum0 = CrossSum(0, cs0, cr0, cg0, ca0, False, False)
-    sum1 = CrossSum(1, cs1, cr1, cg1, ca1, False, False)
+    sum0 = CrossSum(0, cb0, cr0, cg0, ca0, False, False, both_cores=False)
+    sum1 = CrossSum(1, cb1, cr1, cg1, ca1, False, False, both_cores=False)
     sum2 = CrossSum(2, cs2, cr2, cg2, ca2, True, True)
+
+    def core_sum(n, both, arriving, kept):
+        swap = remote(both.at[1 - c], arriving, c_send.at[n], c_recv.at[n], partner)
+        swap.start()
+        closing.append(swap.wait_send)
+        swap.wait_recv()
+        kept[...] = (both[c].astype(F32) + arriving[...].astype(F32)).astype(BF16)
 
     def raw_cross(a, b):
         cross = dot_t(panels[0, a], panels[0, b]) + dot_t(panels[1, a], panels[1, b])
         return cross.astype(BF16).reshape(n_k, part, width)
 
     for i in range(2):
-        cross = raw_cross(2 * i, 2 * i + 1)
-        for kk in range(n_k):
-            cs0[2 * kk + i] = cross[kk]
+        cs0[i] = raw_cross(2 * i, 2 * i + 1)
+    core_sum(6, cs0, cn0, cb0)
     sum0.begin()
     for i in range(2):
         for j in range(2):
-            cross = raw_cross(i, 2 + j)
-            for kk in range(n_k):
-                cs1[2 * kk + i, j] = cross[kk]
+            cs1[i, :, j] = raw_cross(i, 2 + j)
+    core_sum(5, cs1, cn1, cb1)
     sum1.begin()
     sum0.to_share()
     loop(1, n_k, lambda d: diag_gather(d).wait_recv())
@@ -490,9 +497,11 @@
         vmem((2, SPAN, block, width), BF16), vmem((SPAN, block, width), BF16), vmem((rows, width), BF16),
         vmem(sketch.shape, F32),
         vmem((width, width), F32), vmem((n_space, part, width), F32), vmem((n_k, 2, part, width), F32),
-        vmem((n_space, part, width), BF16), vmem((n_space, part, width), BF16),
+        vmem((2, n_k, part, width), BF16), vmem((n_k, part, width), BF16),
+        vmem((n_k, part, width), BF16), vmem((n_k, part, width), BF16),
         vmem((SPAN, part, width), BF16), vmem((n_k, part, width), BF16),
-        vmem((n_space, 2, part, width), BF16), vmem((n_space, 2, part, width), BF16),
+        vmem((2, n_k, 2, part, width), BF16), vmem((n_k, 2, part, width), BF16),
+        vmem((n_k, 2, part, width), BF16), vmem((n_k, 2, part, width), BF16),
         vmem((SPAN, 2, part, width), BF16), vmem((n_k, 2, part, width), BF16),
         vmem((n_space, thin, width), BF16), vmem((n_space, thin, width), BF16),
         vmem((n_group, thin, width), BF16), vmem((n_space, thin, width), BF16),
@@ -504,7 +513,7 @@
         dma((3, PIECES)), dma((3, PIECES)), dma((3,)), dma((3,)), dma((SPAN,)), dma((SPAN,)), dma((4,)),
         dma((n_k,)), dma((n_space,)), dma((SPAN,)), dma((2,)), dma((n_k,)), dma((n_k,)),
         dma((3, n_space)), dma((3, n_space)), dma((3, n_group)), dma((3, n_group)),
-        dma((3, n_space)), dma((3, n_space)), dma((5,)), dma((5,)), dma((2,)), dma((2,)), dma((2,)), dma((2,)),
+        dma((3, n_space)), dma((3, n_space)), dma((8,)), dma((8,)), dma((2,)), dma((2,)), dma((2,)), dma((2,)),
     ]
     return pl.pallas_call(
         functools.partial(kernel, n_space, n_group),

time: 117 us -> 113 us (0.966)
  Pallas kernels: 117 us -> 112 us
    pallas_call x1, Pallas kernels: 117 us -> 112 us  [body(): pl.pallas_call(functools.partial(kernel, n_space, n_group), out_shape=jax...]
where the time goes in v6:
time: 113 us
  Pallas kernels  112 us (99%)
    pallas_call x1, Pallas kernels, body(): pl.pallas_call(functools.partial(kernel, n_space, n_group), out_shape=jax...  112 us

profile of v6, /device:TPU:1, one launch (start us, length us, event | category | flops | bytes accessed | tf_op | source)
XLA Modules:
  0.0 113.3 jit_solution(17851632201310670517)
XLA Ops:
  0.0 112.5 %merge.1 = bf16[1024,256]{1,0:T(8,128)(2,1)S(1)} custom-call(bf16[8192,256]{1,0:T(8,128)(2,1)} %x_hbm.1, f32[3,512,256]{2,1,0:T(8,128)} %sk_hbm.1), custom_call_target="tpu_custom_call" | custom-call | tf_op jit(solution)/shard_map/merge/pallas_call | solution.py:518
  112.5 0.8 copy.4
